TPU v7x, 64 devices: a 2x2x8 block of a 4x4x8 slice. The times are simulated.
64 devices in a mesh: data: 4 (over x, y), stage: 16 (over z, core).
Axes of the slice: x: 2, y: 2, z: 8, core: 2. Of those that a mesh axis runs over, the one named last changes fastest.
The devices are a block of a 4x4x8 slice.
Arguments:
- inputs: bfloat16 [1024, 16, 512], P('data'), parts along dimension 0
- targets: bfloat16 [1024, 16, 512], P('data'), parts along dimension 0
- lengths: int32 [1024], P('data'), parts along dimension 0
- w_in: bfloat16 [16, 512, 2048], P('stage')
- w_rec: bfloat16 [16, 512, 2048], P('stage')
- bias: float32 [16, 2048], P('stage')
- h_init: float32 [16, 1024, 512], P('stage', 'data'), parts along dimension 1
- c_init: float32 [16, 1024, 512], P('stage', 'data'), parts along dimension 1
Outputs:
- output 1: float32 [4], P('data'), parts along dimension 0
- output 2: float32 [64, 512, 2048], P(('data', 'stage')), parts along dimension 0
- output 3: float32 [64, 512, 2048], P(('data', 'stage')), parts along dimension 0
- output 4: float32 [64, 2048], P(('data', 'stage')), parts along dimension 0
- output 5: float32 [16, 1024, 512], P('stage', 'data'), parts along dimension 1
- output 6: float32 [16, 1024, 512], P('stage', 'data'), parts along dimension 1
There are 4 independent parts. A program takes and returns all parts, laid end to end along the dimension named above; an argument that names none is the same for every part.
All inputs are finite; a program needn't handle non-finite values.
Results may differ from a plain program's by a relative error of at most 0.0139054.
Values are sent between devices in bfloat16 or wider.
A program may use at most 768 MiB of HBM per device.

v0:
```python
import jax
import jax.numpy as jnp
from jax import lax
from jax.sharding import PartitionSpec as P

SEG_LEN = 16


def gate_values(pre_act, hidden):
    in_gate = jax.nn.sigmoid(pre_act[:, :hidden])
    forget = jax.nn.sigmoid(pre_act[:, hidden:2 * hidden])
    candidate = jnp.tanh(pre_act[:, 2 * hidden:3 * hidden])
    out_gate = jax.nn.sigmoid(pre_act[:, 3 * hidden:])
    return in_gate, forget, candidate, out_gate


def cell_step(h_prev, c_prev, proj_t, mask_t, w_rec):
    hidden = h_prev.shape[-1]
    pre_act = proj_t + jnp.dot(h_prev, w_rec, preferred_element_type=jnp.float32)
    in_gate, forget, candidate, out_gate = gate_values(pre_act, hidden)
    c_cand = forget * c_prev + in_gate * candidate
    h_cand = (out_gate * jnp.tanh(c_cand)).astype(jnp.bfloat16)
    h_next = jnp.where(mask_t, h_cand, h_prev)
    c_next = jnp.where(mask_t, c_cand, c_prev)
    return h_next, c_next, jnp.where(mask_t, h_cand, jnp.zeros_like(h_cand)), pre_act


def layer_forward(layer_seq, w_in, w_rec, bias, h_init, c_init, mask):
    steps, batch, hidden = layer_seq.shape
    num_segs = steps // SEG_LEN
    seq_segs = layer_seq.reshape(num_segs, SEG_LEN, batch, hidden)
    mask_segs = mask.reshape(num_segs, SEG_LEN, batch, 1)

    def segment(state, seg_data):
        seg_in, seg_mask = seg_data
        in_proj = jnp.einsum('kbh,hg->kbg', seg_in, w_in, preferred_element_type=jnp.float32) + bias

        def step(carry, step_data):
            h_next, c_next, out_t, _ = cell_step(carry[0], carry[1], step_data[0], step_data[1], w_rec)
            return (h_next, c_next), out_t

        end_state, seg_out = lax.scan(step, state, (in_proj, seg_mask))
        return end_state, (seg_out, state[0], state[1])

    start = (h_init.astype(jnp.bfloat16), c_init)
    _, (outputs, h_bounds, c_bounds) = lax.scan(segment, start, (seq_segs, mask_segs))
    return outputs.reshape(steps, batch, hidden), h_bounds, c_bounds


def layer_backward(layer_seq, w_in, w_rec, bias, h_bounds, c_bounds, mask, d_out):
    steps, batch, hidden = layer_seq.shape
    num_segs = steps // SEG_LEN
    seq_segs = layer_seq.reshape(num_segs, SEG_LEN, batch, hidden)
    mask_segs = mask.reshape(num_segs, SEG_LEN, batch, 1)
    dout_segs = d_out.reshape(num_segs, SEG_LEN, batch, hidden)

    def segment(carry, seg_data):
        dh_next, dc_next, gw_in, gw_rec, g_bias = carry
        seg_in, seg_mask, seg_dout, h_start, c_start = seg_data
        in_proj = jnp.einsum('kbh,hg->kbg', seg_in, w_in, preferred_element_type=jnp.float32) + bias

        def step_fwd(state, step_data):
            h_next, c_next, _, pre_act = cell_step(state[0], state[1], step_data[0], step_data[1], w_rec)
            return (h_next, c_next), (state[0], state[1], pre_act)

        _, (h_hist, c_hist, pre_hist) = lax.scan(step_fwd, (h_start, c_start), (in_proj, seg_mask))

        def step_bwd(state, step_data):
            dh_n, dc_n, bias_acc = state
            c_prev, pre_act, mask_t, dout_t = step_data
            in_gate, forget, candidate, out_gate = gate_values(pre_act, hidden)
            tanh_c = jnp.tanh(forget * c_prev + in_gate * candidate)
            d_h = jnp.where(mask_t, dh_n + dout_t, 0.0)
            d_cell = d_h * out_gate * (1.0 - tanh_c * tanh_c) + jnp.where(mask_t, dc_n, 0.0)
            d_pre = jnp.concatenate([
                d_cell * candidate * in_gate * (1.0 - in_gate),
                d_cell * c_prev * forget * (1.0 - forget),
                d_cell * in_gate * (1.0 - candidate * candidate),
                d_h * tanh_c * out_gate * (1.0 - out_gate)], axis=1)
            d_pre_low = d_pre.astype(jnp.bfloat16)
            dh_prev = jnp.where(mask_t, 0.0, dh_n) + jnp.einsum('bg,hg->bh', d_pre_low, w_rec, preferred_element_type=jnp.float32)
            dc_prev = d_cell * forget + jnp.where(mask_t, 0.0, dc_n)
            return (dh_prev, dc_prev, bias_acc + jnp.sum(d_pre, axis=0)), d_pre_low

        (dh_first, dc_first, g_bias), d_pre_hist = lax.scan(step_bwd, (dh_next, dc_next, g_bias), (c_hist, pre_hist, seg_mask, seg_dout), reverse=True)
        gw_in = gw_in + jnp.einsum('kbh,kbg->hg', seg_in, d_pre_hist, preferred_element_type=jnp.float32)
        gw_rec = gw_rec + jnp.einsum('kbh,kbg->hg', h_hist, d_pre_hist, preferred_element_type=jnp.float32)
        d_in = jnp.einsum('kbg,hg->kbh', d_pre_hist, w_in, preferred_element_type=jnp.float32).astype(jnp.bfloat16)
        return (dh_first, dc_first, gw_in, gw_rec, g_bias), d_in

    zero_state = jnp.zeros((batch, hidden), jnp.float32)
    zero_carry = (zero_state, zero_state, jnp.zeros(w_in.shape, jnp.float32), jnp.zeros(w_rec.shape, jnp.float32), jnp.zeros(bias.shape, jnp.float32))
    (dh_init, dc_init, gw_in, gw_rec, g_bias), d_in = lax.scan(segment, zero_carry, (seq_segs, mask_segs, dout_segs, h_bounds, c_bounds), reverse=True)
    return d_in.reshape(steps, batch, hidden), gw_in, gw_rec, g_bias, dh_init, dc_init


def stage_forward(layer_seq, w_in, w_rec, bias, h_init, c_init, mask):
    saved_in, h_saved, c_saved = [], [], []
    for layer_idx in range(w_in.shape[0]):
        saved_in.append(layer_seq)
        layer_seq, h_bounds, c_bounds = layer_forward(layer_seq, w_in[layer_idx], w_rec[layer_idx], bias[layer_idx], h_init[layer_idx], c_init[layer_idx], mask)
        h_saved.append(h_bounds)
        c_saved.append(c_bounds)
    return layer_seq, jnp.stack(saved_in), jnp.stack(h_saved), jnp.stack(c_saved)


def stage_backward(d_seq, saved_in, h_saved, c_saved, w_in, w_rec, bias, mask):
    layer_grads = []
    for layer_idx in reversed(range(w_in.shape[0])):
        d_seq, gw_in, gw_rec, g_bias, grad_h0, grad_c0 = layer_backward(saved_in[layer_idx], w_in[layer_idx], w_rec[layer_idx], bias[layer_idx], h_saved[layer_idx], c_saved[layer_idx], mask, d_seq)
        layer_grads.insert(0, (gw_in, gw_rec, g_bias, grad_h0, grad_c0))
    stacked = [jnp.stack([entry[field] for entry in layer_grads]) for field in range(5)]
    return (d_seq,) + tuple(stacked)


def solution(mesh):
    n_stages = mesh.shape['stage']
    up_perm = [(source, source + 1) for source in range(n_stages - 1)]
    down_perm = [(source + 1, source) for source in range(n_stages - 1)]

    def local(inputs, targets, lengths, w_in, w_rec, bias, h_init, c_init):
        stage_idx = lax.axis_index('stage')
        batch, steps, hidden = inputs.shape
        layers_here = w_in.shape[0]
        num_segs = steps // SEG_LEN
        mask = (jnp.arange(steps)[:, None] < lengths[None, :])[:, :, None]
        zero_seq = jnp.zeros((steps, batch, hidden), jnp.bfloat16)

        def fwd_tick(tick, carry):
            received = carry[0]

            def compute_stage(operands):
                return stage_forward(operands[0], w_in, w_rec, bias, h_init, c_init, mask)

            def keep_stage(operands):
                return operands[1]

            kept = lax.cond(tick == stage_idx, compute_stage, keep_stage, (received, tuple(carry[1:])))
            received = lax.ppermute(kept[0], 'stage', up_perm)
            return (received,) + tuple(kept)

        fwd_carry = (jnp.swapaxes(inputs, 0, 1), zero_seq,
                     jnp.zeros((layers_here, steps, batch, hidden), jnp.bfloat16),
                     jnp.zeros((layers_here, num_segs, batch, hidden), jnp.bfloat16),
                     jnp.zeros((layers_here, num_segs, batch, hidden), jnp.float32))
        fwd_carry = lax.fori_loop(0, n_stages, fwd_tick, fwd_carry)
        top_out, saved_in, h_saved, c_saved = fwd_carry[1:]

        scale = 1.0 / (batch * steps)
        error = top_out.astype(jnp.float32) - jnp.swapaxes(targets, 0, 1).astype(jnp.float32)
        stage_loss = 0.5 * scale * jnp.sum(jnp.where(mask, error * error, 0.0))
        loss = lax.psum(jnp.where(stage_idx == n_stages - 1, stage_loss, 0.0), 'stage')
        d_top = jnp.where(mask, error * scale, 0.0).astype(jnp.bfloat16)

        def bwd_tick(tick, carry):
            received = carry[0]

            def compute_stage(operands):
                return stage_backward(operands[0], saved_in, h_saved, c_saved, w_in, w_rec, bias, mask)

            def keep_stage(operands):
                return operands[1]

            kept = lax.cond(tick == n_stages - 1 - stage_idx, compute_stage, keep_stage, (received, tuple(carry[1:])))
            received = lax.ppermute(kept[0], 'stage', down_perm)
            return (received,) + tuple(kept)

        bwd_carry = (d_top, zero_seq,
                     jnp.zeros(w_in.shape, jnp.float32), jnp.zeros(w_rec.shape, jnp.float32),
                     jnp.zeros(bias.shape, jnp.float32), jnp.zeros(h_init.shape, jnp.float32),
                     jnp.zeros(c_init.shape, jnp.float32))
        bwd_carry = lax.fori_loop(0, n_stages, bwd_tick, bwd_carry)
        return (loss.reshape(1),) + tuple(bwd_carry[2:])

    layer_spec = P(('data', 'stage'))
    return jax.shard_map(
        local, mesh=mesh,
        in_specs=(P('data'), P('data'), P('data'), P('stage'), P('stage'), P('stage'), P('stage', 'data'), P('stage', 'data')),
        out_specs=(P('data'), layer_spec, layer_spec, layer_spec, P('stage', 'data'), P('stage', 'data')),
        check_vma=False)
```

profile of v0, /device:TPU:21, one launch (start us, length us, event | category | flops | bytes accessed | tf_op | source)
XLA Modules:
  0.0 7549.4 jit_solution(160927885564256596)
XLA Ops:
  13.1 1371.7 %while.136 = (s32[]{:T(128)}, bf16[16,256,512]{2,1,0:T(8,128)(2,1)}, bf16[16,256,512]{2,1,0:T(8,128)(2,1)}, bf16[1,16,256,512]{3,2,1,0:T(8,128)(2,1)}, bf16[1,1,...) while((s32[]{:T(128)}, bf16[16,256,512]{2,1,0:T(8,128)(2,1)}, ...), condition=%wide.region_5.6_spmd.clone, body=%wide.region_0.5_spmd.clone.sunk | while | flops 9137950720 | bytes 80788712 | solution.py:146
  18.4 103.5 %collective-permute-done.1 = bf16[16,256,512]{2,1,0:T(8,128)(2,1)} collective-permute-done((bf16[16,256,512]{2,1,0:T(8,128)(2,1)}, bf16[16,256,512]{2,1,0:T(8,128)(2,1)}, u32[]{:S(2)}, u32[]{:S(2)}) %collective-permute-start.1) | collective-permute-done | bytes 4194336 | tf_op jit(solution)/shard_map/while/body/eval_jaxpr/ppermute | solution.py:139
  121.9 96.0 %conditional.6 = ((bf16[16,256,512]{2,1,0:T(8,128)(2,1)}, bf16[1,16,256,512]{3,2,1,0:T(8,128)(2,1)}, bf16[1,1,256,512]{3,2,1,0:T(8,128)(2,1)S(1)}, f32[1,1,256,512]{3,2,1,0:T(8,128)})) conditional(s32[]{:T(128)} %convert_element_type.122, (bf16[16,256,512]{2,1,0:T(8,128)(2,1)}, bf16[1,16,256,512]{3,2,1,0:T(8,128)(2,1)}, ...), branch_computations={%region_1.0_spmd, %region_2.4_spmd} | conditional | flops 9137950720 | bytes 63994828 | solution.py:138
  139.8 72.8 while.133
  219.9 45.4 collective-permute-done.1
  265.3 100.5 %collective-permute-start.1 = (bf16[16,256,512]{2,1,0:T(8,128)(2,1)}, bf16[16,256,512]{2,1,0:T(8,128)(2,1)}, u32[]{:S(2)}, u32[]{:S(2)}) collective-permute-start(bf16[16,256,512]{2,1,0:T(8,128)(2,1)} %get-tuple-element.1871), channel_id=1, source_target_pairs={{0,1},{1,2},{2,3},{3,4},{4,5},{5,6},{6,7},{7,8},{8,9},{9,10},{10,1... | collective-permute-start | bytes 12582920 | tf_op jit(solution)/shard_map/while/body/eval_jaxpr/ppermute | solution.py:139
  365.9 45.4 collective-permute-done.1
  415.7 45.4 collective-permute-done.1
  574.9 98.0 %collective-permute-start.1 = (bf16[16,256,512]{2,1,0:T(8,128)(2,1)}, bf16[16,256,512]{2,1,0:T(8,128)(2,1)}, u32[]{:S(2)}, u32[]{:S(2)}) collective-permute-start(bf16[16,256,512]{2,1,0:T(8,128)(2,1)} %get-tuple-element.1871), channel_id=1, source_target_pairs={{0,1},{1,2},{2,3},{3,4},{4,5},{5,6},{6,7},{7,8},{8,9},{9,10},{10,1... | collective-permute-start | bytes 12582920 | tf_op jit(solution)/shard_map/while/body/eval_jaxpr/ppermute | solution.py:139
  672.9 45.4 collective-permute-done.1
  882.0 98.0 %collective-permute-start.1 = (bf16[16,256,512]{2,1,0:T(8,128)(2,1)}, bf16[16,256,512]{2,1,0:T(8,128)(2,1)}, u32[]{:S(2)}, u32[]{:S(2)}) collective-permute-start(bf16[16,256,512]{2,1,0:T(8,128)(2,1)} %get-tuple-element.1871), channel_id=1, source_target_pairs={{0,1},{1,2},{2,3},{3,4},{4,5},{5,6},{6,7},{7,8},{8,9},{9,10},{10,1... | collective-permute-start | bytes 12582920 | tf_op jit(solution)/shard_map/while/body/eval_jaxpr/ppermute | solution.py:139
  1189.1 99.2 %collective-permute-start.1 = (bf16[16,256,512]{2,1,0:T(8,128)(2,1)}, bf16[16,256,512]{2,1,0:T(8,128)(2,1)}, u32[]{:S(2)}, u32[]{:S(2)}) collective-permute-start(bf16[16,256,512]{2,1,0:T(8,128)(2,1)} %get-tuple-element.1871), channel_id=1, source_target_pairs={{0,1},{1,2},{2,3},{3,4},{4,5},{5,6},{6,7},{7,8},{8,9},{9,10},{10,1... | collective-permute-start | bytes 12582920 | tf_op jit(solution)/shard_map/while/body/eval_jaxpr/ppermute | solution.py:139
  1400.3 6118.5 %while.137 = (s32[]{:T(128)}, bf16[16,256,512]{2,1,0:T(8,128)(2,1)}, bf16[16,256,512]{2,1,0:T(8,128)(2,1)}, f32[1,512,2048]{1,2,0:T(8,128)}, f32[1,512,2048]{2,1...) while((s32[]{:T(128)}, bf16[16,256,512]{2,1,0:T(8,128)(2,1)}, ...), condition=%wide.region_16.17_spmd.clone, body=%wide.region_8.16_spmd.clone.sunk | while | flops 35465338880 | bytes 266225488 | solution.py:172
  1402.5 61.6 collective-permute-done
  1466.0 48.9 collective-permute-done
  1516.9 141.0 %collective-permute-done = bf16[16,256,512]{2,1,0:T(8,128)(2,1)} collective-permute-done((bf16[16,256,512]{2,1,0:T(8,128)(2,1)}, bf16[16,256,512]{2,1,0:T(8,128)(2,1)}, u32[]{:S(2)}, u32[]{:S(2)}) %collective-permute-start) | collective-permute-done | bytes 4194336 | tf_op jit(solution)/shard_map/while/body/eval_jaxpr/ppermute | solution.py:165
  1659.9 48.9 collective-permute-done
  1710.8 61.6 collective-permute-done
  1774.3 48.9 collective-permute-done
  1825.2 141.0 %collective-permute-done = bf16[16,256,512]{2,1,0:T(8,128)(2,1)} collective-permute-done((bf16[16,256,512]{2,1,0:T(8,128)(2,1)}, bf16[16,256,512]{2,1,0:T(8,128)(2,1)}, u32[]{:S(2)}, u32[]{:S(2)}) %collective-permute-start) | collective-permute-done | bytes 4194336 | tf_op jit(solution)/shard_map/while/body/eval_jaxpr/ppermute | solution.py:165
  1968.2 49.1 collective-permute-done
  2019.2 61.4 collective-permute-done
  2082.6 49.1 collective-permute-done
  2133.6 140.8 %collective-permute-done = bf16[16,256,512]{2,1,0:T(8,128)(2,1)} collective-permute-done((bf16[16,256,512]{2,1,0:T(8,128)(2,1)}, bf16[16,256,512]{2,1,0:T(8,128)(2,1)}, u32[]{:S(2)}, u32[]{:S(2)}) %collective-permute-start) | collective-permute-done | bytes 4194336 | tf_op jit(solution)/shard_map/while/body/eval_jaxpr/ppermute | solution.py:165
  2276.4 49.1 collective-permute-done
  2327.5 61.4 collective-permute-done
  2390.8 4472.2 %collective-permute-done = bf16[16,256,512]{2,1,0:T(8,128)(2,1)} collective-permute-done((bf16[16,256,512]{2,1,0:T(8,128)(2,1)}, bf16[16,256,512]{2,1,0:T(8,128)(2,1)}, u32[]{:S(2)}, u32[]{:S(2)}) %collective-permute-start) | collective-permute-done | bytes 4194336 | tf_op jit(solution)/shard_map/while/body/eval_jaxpr/ppermute | solution.py:165
  6863.0 319.0 %conditional.7 = ((bf16[16,256,512]{2,1,0:T(8,128)(2,1)}, f32[1,512,2048]{1,2,0:T(8,128)}, f32[1,512,2048]{2,1,0:T(8,128)}, f32[1,2048]{1,0:T(1,128)S(1)}, f32[1...) conditional(s32[]{:T(128)} %convert_element_type.123, (bf16[16,256,512]{2,1,0:T(8,128)(2,1)}, ...), branch_computations={%region_9.9_spmd, %region_10.15_spmd} | conditional | flops 35465338880 | bytes 249431552 | solution.py:164
  6881.9 106.6 %while.134 = (s32[]{:T(128)}, bf16[256,512]{1,0:T(8,128)(2,1)S(1)}, f32[256,512]{1,0:T(8,128)S(1)}, bf16[16,256,512]{2,1,0:T(8,128)(2,1)}, f32[16,256,512]{2,1,0...) while((s32[]{:T(128)}, bf16[256,512]{1,0:T(8,128)(2,1)S(1)}, ...), condition=%wide.region_12.11_spmd, body=%wide.region_11.10_spmd.sunk | while | flops 539492352 | bytes 14944873 | solution.py:66
  6994.5 146.1 %while.135 = (s32[]{:T(128)}, f32[256,512]{1,0:T(8,128)S(1)}, f32[256,512]{1,0:T(8,128)S(1)}, f32[2048]{0:T(1024)S(1)}, bf16[16,256,2048]{2,1,0:T(8,128)(2,1)}, ...) while((s32[]{:T(128)}, f32[256,512]{1,0:T(8,128)S(1)}, ...), condition=%wide.region_15.14_spmd.clone, body=%wide.region_13.13_spmd.clone.sunk | while | flops 555616256 | bytes 27297192 | solution.py:85
  7184.0 47.9 collective-permute-done
  7231.9 280.1 %collective-permute-start = (bf16[16,256,512]{2,1,0:T(8,128)(2,1)}, bf16[16,256,512]{2,1,0:T(8,128)(2,1)}, u32[]{:S(2)}, u32[]{:S(2)}) collective-permute-start(bf16[16,256,512]{2,1,0:T(8,128)(2,1)} %get-tuple-element.1919), channel_id=1, source_target_pairs={{1,0},{2,1},{3,2},{4,3},{5,4},{6,5},{7,6},{8,7},{9,8},{10,9},{11,1... | collective-permute-start | bytes 12582920 | tf_op jit(solution)/shard_map/while/body/eval_jaxpr/ppermute | solution.py:165
  (471 shorter events, 1101.6 us)
Async XLA Ops:
  13.3 108.6 %collective-permute-start.1 = (bf16[16,256,512]{2,1,0:T(8,128)(2,1)}, bf16[16,256,512]{2,1,0:T(8,128)(2,1)}, u32[]{:S(2)}, u32[]{:S(2)}) collective-permute-start(bf16[16,256,512]{2,1,0:T(8,128)(2,1)} %get-tuple-element.1871), channel_id=1, source_target_pairs={{0,1},{1,2},{2,3},{3,4},{4,5},{5,6},{6,7},{7,8},{8,9},{9,10},{10,1... | collective-permute-start | bytes 12582920 | tf_op jit(solution)/shard_map/while/body/eval_jaxpr/ppermute | solution.py:139
  218.0 47.4 collective-permute-start.1
  265.3 145.9 %collective-permute-start.1 = (bf16[16,256,512]{2,1,0:T(8,128)(2,1)}, bf16[16,256,512]{2,1,0:T(8,128)(2,1)}, u32[]{:S(2)}, u32[]{:S(2)}) collective-permute-start(bf16[16,256,512]{2,1,0:T(8,128)(2,1)} %get-tuple-element.1871), channel_id=1, source_target_pairs={{0,1},{1,2},{2,3},{3,4},{4,5},{5,6},{6,7},{7,8},{8,9},{9,10},{10,1... | collective-permute-start | bytes 12582920 | tf_op jit(solution)/shard_map/while/body/eval_jaxpr/ppermute | solution.py:139
  411.3 49.8 collective-permute-start.1
  461.1 64.0 collective-permute-start.1
  525.1 49.8 collective-permute-start.1
  574.9 143.4 %collective-permute-start.1 = (bf16[16,256,512]{2,1,0:T(8,128)(2,1)}, bf16[16,256,512]{2,1,0:T(8,128)(2,1)}, u32[]{:S(2)}, u32[]{:S(2)}) collective-permute-start(bf16[16,256,512]{2,1,0:T(8,128)(2,1)} %get-tuple-element.1871), channel_id=1, source_target_pairs={{0,1},{1,2},{2,3},{3,4},{4,5},{5,6},{6,7},{7,8},{8,9},{9,10},{10,1... | collective-permute-start | bytes 12582920 | tf_op jit(solution)/shard_map/while/body/eval_jaxpr/ppermute | solution.py:139
  718.3 49.8 collective-permute-start.1
  768.2 64.0 collective-permute-start.1
  832.2 49.8 collective-permute-start.1
  882.0 143.4 %collective-permute-start.1 = (bf16[16,256,512]{2,1,0:T(8,128)(2,1)}, bf16[16,256,512]{2,1,0:T(8,128)(2,1)}, u32[]{:S(2)}, u32[]{:S(2)}) collective-permute-start(bf16[16,256,512]{2,1,0:T(8,128)(2,1)} %get-tuple-element.1871), channel_id=1, source_target_pairs={{0,1},{1,2},{2,3},{3,4},{4,5},{5,6},{6,7},{7,8},{8,9},{9,10},{10,1... | collective-permute-start | bytes 12582920 | tf_op jit(solution)/shard_map/while/body/eval_jaxpr/ppermute | solution.py:139
  1025.4 49.8 collective-permute-start.1
  1075.3 63.9 collective-permute-start.1
  1139.2 49.8 collective-permute-start.1
  1189.1 144.6 %collective-permute-start.1 = (bf16[16,256,512]{2,1,0:T(8,128)(2,1)}, bf16[16,256,512]{2,1,0:T(8,128)(2,1)}, u32[]{:S(2)}, u32[]{:S(2)}) collective-permute-start(bf16[16,256,512]{2,1,0:T(8,128)(2,1)} %get-tuple-element.1871), channel_id=1, source_target_pairs={{0,1},{1,2},{2,3},{3,4},{4,5},{5,6},{6,7},{7,8},{8,9},{9,10},{10,1... | collective-permute-start | bytes 12582920 | tf_op jit(solution)/shard_map/while/body/eval_jaxpr/ppermute | solution.py:139
  1333.7 51.1 collective-permute-start.1
  1400.6 63.5 collective-permute-start
  1464.1 50.9 collective-permute-start
  1515.0 143.0 %collective-permute-start = (bf16[16,256,512]{2,1,0:T(8,128)(2,1)}, bf16[16,256,512]{2,1,0:T(8,128)(2,1)}, u32[]{:S(2)}, u32[]{:S(2)}) collective-permute-start(bf16[16,256,512]{2,1,0:T(8,128)(2,1)} %get-tuple-element.1919), channel_id=1, source_target_pairs={{1,0},{2,1},{3,2},{4,3},{5,4},{6,5},{7,6},{8,7},{9,8},{10,9},{11,1... | collective-permute-start | bytes 12582920 | tf_op jit(solution)/shard_map/while/body/eval_jaxpr/ppermute | solution.py:165
  1657.9 50.9 collective-permute-start
  1708.8 63.5 collective-permute-start
  1772.3 50.9 collective-permute-start
  1823.2 143.0 %collective-permute-start = (bf16[16,256,512]{2,1,0:T(8,128)(2,1)}, bf16[16,256,512]{2,1,0:T(8,128)(2,1)}, u32[]{:S(2)}, u32[]{:S(2)}) collective-permute-start(bf16[16,256,512]{2,1,0:T(8,128)(2,1)} %get-tuple-element.1919), channel_id=1, source_target_pairs={{1,0},{2,1},{3,2},{4,3},{5,4},{6,5},{7,6},{8,7},{9,8},{10,9},{11,1... | collective-permute-start | bytes 12582920 | tf_op jit(solution)/shard_map/while/body/eval_jaxpr/ppermute | solution.py:165
  1966.2 51.1 collective-permute-start
  2017.3 63.3 collective-permute-start
  2080.6 51.1 collective-permute-start
  2131.7 142.8 %collective-permute-start = (bf16[16,256,512]{2,1,0:T(8,128)(2,1)}, bf16[16,256,512]{2,1,0:T(8,128)(2,1)}, u32[]{:S(2)}, u32[]{:S(2)}) collective-permute-start(bf16[16,256,512]{2,1,0:T(8,128)(2,1)} %get-tuple-element.1919), channel_id=1, source_target_pairs={{1,0},{2,1},{3,2},{4,3},{5,4},{6,5},{7,6},{8,7},{9,8},{10,9},{11,1... | collective-permute-start | bytes 12582920 | tf_op jit(solution)/shard_map/while/body/eval_jaxpr/ppermute | solution.py:165
  2274.5 51.1 collective-permute-start
  2325.5 63.3 collective-permute-start
  2388.9 4474.1 %collective-permute-start = (bf16[16,256,512]{2,1,0:T(8,128)(2,1)}, bf16[16,256,512]{2,1,0:T(8,128)(2,1)}, u32[]{:S(2)}, u32[]{:S(2)}) collective-permute-start(bf16[16,256,512]{2,1,0:T(8,128)(2,1)} %get-tuple-element.1919), channel_id=1, source_target_pairs={{1,0},{2,1},{3,2},{4,3},{5,4},{6,5},{7,6},{8,7},{9,8},{10,9},{11,1... | collective-permute-start | bytes 12582920 | tf_op jit(solution)/shard_map/while/body/eval_jaxpr/ppermute | solution.py:165
  7182.0 49.9 collective-permute-start
  7231.9 286.9 %collective-permute-start = (bf16[16,256,512]{2,1,0:T(8,128)(2,1)}, bf16[16,256,512]{2,1,0:T(8,128)(2,1)}, u32[]{:S(2)}, u32[]{:S(2)}) collective-permute-start(bf16[16,256,512]{2,1,0:T(8,128)(2,1)} %get-tuple-element.1919), channel_id=1, source_target_pairs={{1,0},{2,1},{3,2},{4,3},{5,4},{6,5},{7,6},{8,7},{9,8},{10,9},{11,1... | collective-permute-start | bytes 12582920 | tf_op jit(solution)/shard_map/while/body/eval_jaxpr/ppermute | solution.py:165
  (14 other events, 143.6 us)
where the time goes:
time: 7550 us
  waiting for transfers between devices  6270 us (83%)
  starting transfers between devices  800 us (11%)
  matrix products  232 us (3%)
  other arithmetic  123 us (2%)
  local copies, waits for them, and re-layouts  92.4 us (1%)
    ppermute x16, waiting for transfers between devices, bwd_tick(): received = lax.ppermute(kept[0], 'stage', down_perm)  5490 us
    ppermute x16, waiting for transfers between devices, fwd_tick(): received = lax.ppermute(kept[0], 'stage', up_perm)  785 us
    ppermute x16, starting transfers between devices, fwd_tick(): received = lax.ppermute(kept[0], 'stage', up_perm)  491 us
    ppermute x16, starting transfers between devices, bwd_tick(): received = lax.ppermute(kept[0], 'stage', down_perm)  309 us
  transfers between devices with their start and end apart: 32, of which 32 were waited for; matrix products, arithmetic and copies ran while one was open for 0% of the time, Pallas kernels for 0%

commit v1 on v0

v1 whole, which is shorter than its diff:
```python
import functools

import jax
import jax.numpy as jnp
from jax import lax
from jax.experimental import pallas as pl
from jax.experimental.pallas import tpu as pltpu
from jax.sharding import PartitionSpec as P

F32 = jnp.float32
BF16 = jnp.bfloat16
W_STEPS = 4


def mm(lhs, rhs):
    return jnp.dot(lhs, rhs, preferred_element_type=F32)


def mm_t(lhs, rhs):
    return lax.dot_general(lhs, rhs, (((0,), (0,)), ((), ())), preferred_element_type=F32)


def sigmoid(value):
    return 0.5 * jnp.tanh(0.5 * value) + 0.5


def kernel(last, steps, rows, hidden,
           inputs_ref, targets_ref, lens_ref, w_in_ref, w_rec_ref, bias_ref, h0_ref, c0_ref,
           loss_ref, g_in_ref, g_rec_ref, g_bias_ref, dh0_ref, dc0_ref,
           gates, dz, hist, seq, dout, win, wrec, win_t, wrec_t, acc_in, acc_rec, ring_h, ring_d, dhs, dcs, lens,
           loss_acc, loss_buf, g_bias,
           f_recv, f_send, b_recv, b_send, loss_recv, loss_send, local_sem, out_sem):
    stage = lax.axis_index('stage')
    lo, hi = stage > 0, stage < last
    first, top = stage == 0, stage == last
    span = W_STEPS * rows
    batch = 2 * rows
    n_pieces = steps // W_STEPS
    scale = 1.0 / (batch * steps)

    def at_step(step):
        return pl.ds(pl.multiple_of(step * rows, rows), rows)

    def f_copy(group, step):
        slot = lax.rem(step, 2)
        return pltpu.make_async_remote_copy(
            src_ref=ring_h.at[group, slot], dst_ref=seq.at[group, at_step(step), :],
            send_sem=f_send.at[group, slot], recv_sem=f_recv.at[group, step],
            device_id={'stage': stage + 1}, device_id_type=pl.DeviceIdType.MESH)

    def b_copy(group, step):
        slot = lax.rem(step, 2)
        return pltpu.make_async_remote_copy(
            src_ref=ring_d.at[group, slot], dst_ref=dout.at[group, at_step(step), :],
            send_sem=b_send.at[group, slot], recv_sem=b_recv.at[group, step],
            device_id={'stage': stage - 1}, device_id_type=pl.DeviceIdType.MESH)

    def loss_copy():
        return pltpu.make_async_remote_copy(
            src_ref=loss_buf, dst_ref=loss_buf, send_sem=loss_send, recv_sem=loss_recv,
            device_id={'stage': stage - 1}, device_id_type=pl.DeviceIdType.MESH)

    def load(src, dst, sem):
        return pltpu.make_async_copy(src, dst, local_sem.at[sem])

    loads = []
    for q in range(4):
        cols = pl.ds(q * hidden, hidden)
        loads.append(load(w_in_ref.at[:, cols], win.at[q], 0 + q))
        loads.append(load(w_rec_ref.at[:, cols], wrec.at[q], 4 + q))
    loads.append(load(c0_ref.at[pl.ds(0, rows), :], dhs.at[1], 8))
    loads.append(load(c0_ref.at[pl.ds(rows, rows), :], dcs.at[1], 9))
    loads.append(load(c0_ref.at[pl.ds(0, rows), :], dhs.at[0], 10))
    loads.append(load(h0_ref.at[pl.ds(0, rows), :], gates.at[0, :, pl.ds(0, hidden)], 11))
    loads.append(load(h0_ref.at[pl.ds(rows, rows), :], gates.at[1, :, pl.ds(0, hidden)], 12))

    def land(src, group):
        return load(src.at[pl.ds(group * rows * steps, rows * steps), :],
                    dz.at[group, pl.ds(0, rows * steps), :], 13 + group)

    @pl.when(first)
    def _():
        for group in range(2):
            land(inputs_ref, group).start()

    for copy in loads:
        copy.start()

    @pl.when(top)
    def _():
        for group in range(2):
            land(targets_ref, group).start()

    barrier = pltpu.get_barrier_semaphore()

    @pl.when(lo)
    def _():
        pl.semaphore_signal(barrier, inc=1, device_id={'stage': stage - 1}, device_id_type=pl.DeviceIdType.MESH)

    @pl.when(hi)
    def _():
        pl.semaphore_signal(barrier, inc=1, device_id={'stage': stage + 1}, device_id_type=pl.DeviceIdType.MESH)

    for group in range(2):
        row = lens_ref[group:group + 1, :].astype(F32)
        lens[group] = jnp.broadcast_to(row, (128, rows)).T

    loss_acc[...] = jnp.zeros_like(loss_acc)
    g_bias[...] = jnp.zeros_like(g_bias)

    @pl.when(jnp.logical_and(lo, hi))
    def _():
        pl.semaphore_wait(barrier, 2)

    @pl.when(jnp.logical_or(first, top))
    def _():
        pl.semaphore_wait(barrier, 1)

    def time_major(group, dst):
        size = 16 * steps
        out_row = lax.broadcasted_iota(jnp.int32, (size, size), 0)
        in_row = lax.broadcasted_iota(jnp.int32, (size, size), 1)
        step_of, row_of = lax.div(out_row, 16), lax.rem(out_row, 16)
        permute = (in_row == row_of * steps + step_of).astype(F32).astype(BF16)

        def block(idx, _):
            piece = dz[group, pl.ds(pl.multiple_of(idx * size, size), size), :]
            moved = mm(permute, piece).astype(BF16)
            for step in range(steps):
                dst[group, pl.ds(pl.multiple_of(step * rows + idx * 16, 16), 16), :] = moved[step * 16:(step + 1) * 16]
            return 0

        lax.fori_loop(0, rows // 16, block, 0)

    def set_up():
        def turn(q, _):
            win_t[q] = win[q].T
            wrec_t[q] = wrec[q].T
            acc_in[q] = jnp.zeros((hidden, hidden), F32)
            acc_rec[q] = jnp.zeros((hidden, hidden), F32)
            return 0

        lax.fori_loop(0, 4, turn, 0)

    @pl.when(first)
    def _():
        land(inputs_ref, 0).wait()
        time_major(0, seq)

    for copy in loads:
        copy.wait()
    for group in range(2):
        h_start = gates[group, :, 0:hidden].astype(BF16)
        hist[group, 0:rows, :] = h_start
        ring_h[group, 1] = h_start

    @pl.when(top)
    def _():
        for group in range(2):
            land(targets_ref, group).wait()
            time_major(group, dout)

    early = stage >= (last + 1) // 2

    @pl.when(early)
    def _():
        set_up()

    def pre_act(x, h, q):
        return mm(x, win[q]) + mm(h, wrec[q]) + bias_ref[:, q * hidden:(q + 1) * hidden]

    def forward(group, step, c_ref):
        @pl.when(lo)
        def _():
            f_copy(group, step).wait_recv()

        slot = lax.rem(step, 2)
        x = seq[group, at_step(step), :]
        h = ring_h[group, 1 - slot]
        in_gate = sigmoid(pre_act(x, h, 0))
        cand = jnp.tanh(pre_act(x, h, 2))
        forget = sigmoid(pre_act(x, h, 1))
        c_new = forget * c_ref[...] + in_gate * cand
        c_ref[...] = c_new
        tanh_c = jnp.tanh(c_new)
        out_gate = sigmoid(pre_act(x, h, 3))
        live = jnp.tile(lens[group] > step.astype(F32), (1, hidden // 128))
        h_new = jnp.where(live, out_gate * tanh_c, 0.0).astype(BF16)

        @pl.when(jnp.logical_and(hi, step >= 2))
        def _():
            f_copy(group, step - 2).wait_send()

        ring_h[group, slot] = h_new

        @pl.when(hi)
        def _():
            f_copy(group, step).start()

        @pl.when(top)
        def _():
            goal = dout[group, at_step(step), :].astype(F32)
            out = ring_h[group, slot].astype(F32)
            now = jnp.tile(lens[group] > step.astype(F32), (1, hidden // 128))
            error = jnp.where(now, out - goal, 0.0)
            loss_acc[...] += jnp.sum((error * error).reshape(rows // 8, 8, hidden), axis=0)
            dout[group, at_step(step), :] = (error * scale).astype(BF16)

    def recompute(group, step, slot, c_ref):
        x = seq[group, at_step(step), :]
        h = hist[group, at_step(step), :]
        in_gate = sigmoid(pre_act(x, h, 0))
        gates[slot, :, 0:hidden] = in_gate
        cand = jnp.tanh(pre_act(x, h, 2))
        gates[slot, :, 2 * hidden:3 * hidden] = cand
        forget = sigmoid(pre_act(x, h, 1))
        gates[slot, :, hidden:2 * hidden] = forget
        c_prev = c_ref[...]
        gates[slot, :, 4 * hidden:5 * hidden] = c_prev
        c_new = forget * c_prev + in_gate * cand
        c_ref[...] = c_new
        out_gate = sigmoid(pre_act(x, h, 3))
        gates[slot, :, 3 * hidden:4 * hidden] = out_gate
        live = jnp.tile(lens[group] > step.astype(F32), (1, hidden // 128))
        hist[group, at_step(step + 1), :] = jnp.where(live, out_gate * jnp.tanh(c_new), 0.0).astype(BF16)

    def backward(group, step, slot, place):
        @pl.when(hi)
        def _():
            b_copy(group, step).wait_recv()

        d_h = dhs[group] + dout[group, at_step(step), :].astype(F32)
        in_gate = gates[slot, :, 0:hidden]
        forget = gates[slot, :, hidden:2 * hidden]
        cand = gates[slot, :, 2 * hidden:3 * hidden]
        out_gate = gates[slot, :, 3 * hidden:4 * hidden]
        c_prev = gates[slot, :, 4 * hidden:5 * hidden]
        tanh_c = jnp.tanh(forget * c_prev + in_gate * cand)
        d_cell = d_h * out_gate * (1.0 - tanh_c * tanh_c) + dcs[group]
        dcs[group] = d_cell * forget
        parts = [
            d_cell * cand * in_gate * (1.0 - in_gate),
            d_cell * c_prev * forget * (1.0 - forget),
            d_cell * in_gate * (1.0 - cand * cand),
            d_h * tanh_c * out_gate * (1.0 - out_gate)]
        low = []
        for q in range(4):
            g_bias[q] += jnp.sum(parts[q].reshape(rows // 8, 8, hidden), axis=0)
            low.append(parts[q].astype(BF16))
            dz[q, at_step(place), :] = low[q]
        ring_slot = lax.rem(step, 2)

        @pl.when(jnp.logical_and(lo, step < steps - 2))
        def _():
            b_copy(group, step + 2).wait_send()

        d_in = mm(low[0], win_t[0]) + mm(low[1], win_t[1]) + mm(low[2], win_t[2]) + mm(low[3], win_t[3])
        ring_d[group, ring_slot] = d_in.astype(BF16)

        @pl.when(lo)
        def _():
            b_copy(group, step).start()

        dhs[group] = mm(low[0], wrec_t[0]) + mm(low[1], wrec_t[1]) + mm(low[2], wrec_t[2]) + mm(low[3], wrec_t[3])

    def weight_piece(group, piece, q, place):
        here = pl.ds(pl.multiple_of(piece * span, span), span)
        there = pl.ds(pl.multiple_of(place * rows, span), span)
        d_part = dz[q, there, :]
        acc_in[q] += mm_t(seq[group, here, :], d_part)
        acc_rec[q] += mm_t(hist[group, here, :], d_part)

    def place_of(step):
        tick_piece = n_pieces - 1 - lax.div(step, W_STEPS)
        return lax.rem(tick_piece + n_pieces, n_pieces + 1) * W_STEPS + lax.rem(step, W_STEPS)

    def phase_1(step, _):
        forward(0, step, dhs.at[1])
        return 0

    lax.fori_loop(0, steps, phase_1, 0)

    @pl.when(first)
    def _():
        land(inputs_ref, 1).wait()
        time_major(1, seq)

    again = load(c0_ref.at[pl.ds(rows, rows), :], dhs.at[1], 8)
    again.start()

    def phase_2(step, _):
        recompute(0, step, step, dhs.at[0])
        forward(1, step, dcs.at[1])
        return 0

    lax.fori_loop(0, steps, phase_2, 0)
    again.wait()

    @pl.when(top)
    def _():
        total = jnp.sum(loss_acc[...]) * (0.5 * scale)
        loss_buf[...] = jnp.full(loss_buf.shape, total, F32)
        loss_copy().start()

    @pl.when(jnp.logical_not(early))
    def _():
        set_up()

    dhs[0] = jnp.zeros((rows, hidden), F32)
    dcs[0] = jnp.zeros((rows, hidden), F32)

    def phase_3(tick, _):
        recompute(1, tick, steps - tick, dhs.at[1])
        backward(0, steps - 1 - tick, steps - 1 - tick, steps - 1 - tick)
        return 0

    lax.fori_loop(0, steps, phase_3, 0)

    def put(src, dst, sem):
        return pltpu.make_async_copy(src, dst, out_sem.at[sem])

    stores = [put(dhs.at[0], dh0_ref.at[pl.ds(0, rows), :], 0), put(dcs.at[0], dc0_ref.at[pl.ds(0, rows), :], 1)]
    stores[0].start()
    stores[1].start()

    @pl.when(hi)
    def _():
        loss_copy().wait_recv()

        @pl.when(lo)
        def _():
            loss_copy().start()

    loss_ref[0] = loss_buf[0, 0]
    dhs[1] = jnp.zeros((rows, hidden), F32)
    dcs[1] = jnp.zeros((rows, hidden), F32)

    def phase_4(tick, _):
        step = steps - 1 - tick
        backward(1, step, steps - step, place_of(step))
        piece = lax.div(tick, W_STEPS)
        weight_piece(0, piece, lax.rem(tick, W_STEPS), piece * W_STEPS)
        return 0

    lax.fori_loop(0, steps, phase_4, 0)
    stores += [put(dhs.at[1], dh0_ref.at[pl.ds(rows, rows), :], 2), put(dcs.at[1], dc0_ref.at[pl.ds(rows, rows), :], 3)]
    stores[2].start()
    stores[3].start()
    for q in range(4):
        g_bias_ref[:, q * hidden:(q + 1) * hidden] = jnp.sum(g_bias[q], axis=0, keepdims=True)

    for q in range(4):
        def piece_loop(piece, _, q=q):
            weight_piece(1, piece, q, place_of(piece * W_STEPS))
            return 0

        lax.fori_loop(0, n_pieces, piece_loop, 0)
        cols = pl.ds(q * hidden, hidden)
        stores += [put(acc_in.at[q], g_in_ref.at[:, cols], 4 + 2 * q), put(acc_rec.at[q], g_rec_ref.at[:, cols], 5 + 2 * q)]
        stores[-2].start()
        stores[-1].start()

    for copy in stores:
        copy.wait()

    @pl.when(hi)
    def _():
        for group in range(2):
            for step in (steps - 2, steps - 1):
                f_copy(group, step).wait_send()

    @pl.when(lo)
    def _():
        for group in range(2):
            for step in (1, 0):
                b_copy(group, step).wait_send()
        loss_copy().wait_send()


def solution(mesh):
    last = mesh.shape['stage'] - 1

    def local(inputs, targets, lengths, w_in, w_rec, bias, h_init, c_init):
        batch, steps, hidden = inputs.shape
        rows = batch // 2
        wide = 4 * hidden
        any_spec = pl.BlockSpec(memory_space=pl.ANY)
        vmem_spec = pl.BlockSpec(memory_space=pltpu.VMEM)
        dma = pltpu.SemaphoreType.DMA
        loss, g_in, g_rec, g_bias, dh0, dc0 = pl.pallas_call(
            functools.partial(kernel, last, steps, rows, hidden),
            out_shape=(
                jax.ShapeDtypeStruct((1,), F32),
                jax.ShapeDtypeStruct((hidden, wide), F32),
                jax.ShapeDtypeStruct((hidden, wide), F32),
                jax.ShapeDtypeStruct((1, wide), F32),
                jax.ShapeDtypeStruct((batch, hidden), F32),
                jax.ShapeDtypeStruct((batch, hidden), F32)),
            in_specs=[any_spec, any_spec, vmem_spec, any_spec, any_spec, vmem_spec, any_spec, any_spec],
            out_specs=(pl.BlockSpec(memory_space=pltpu.SMEM), any_spec, any_spec, vmem_spec, any_spec, any_spec),
            scratch_shapes=[
                pltpu.VMEM((steps + 1, rows, 5 * hidden), F32),
                pltpu.VMEM((4, (steps + W_STEPS) * rows, hidden), BF16),
                pltpu.VMEM((2, (steps + 1) * rows, hidden), BF16),
                pltpu.VMEM((2, steps * rows, hidden), BF16),
                pltpu.VMEM((2, steps * rows, hidden), BF16),
                pltpu.VMEM((4, hidden, hidden), BF16),
                pltpu.VMEM((4, hidden, hidden), BF16),
                pltpu.VMEM((4, hidden, hidden), BF16),
                pltpu.VMEM((4, hidden, hidden), BF16),
                pltpu.VMEM((4, hidden, hidden), F32),
                pltpu.VMEM((4, hidden, hidden), F32),
                pltpu.VMEM((2, 2, rows, hidden), BF16),
                pltpu.VMEM((2, 2, rows, hidden), BF16),
                pltpu.VMEM((2, rows, hidden), F32),
                pltpu.VMEM((2, rows, hidden), F32),
                pltpu.VMEM((2, rows, 128), F32),
                pltpu.VMEM((8, hidden), F32),
                pltpu.VMEM((8, 128), F32),
                pltpu.VMEM((4, 8, hidden), F32),
                dma((2, steps)), dma((2, 2)), dma((2, steps)), dma((2, 2)), dma, dma, dma((15,)), dma((12,))],
            compiler_params=pltpu.CompilerParams(
                collective_id=0, has_side_effects=True, vmem_limit_bytes=67043328),
        )(inputs.reshape(batch * steps, hidden), targets.reshape(batch * steps, hidden), lengths.reshape(2, rows),
          w_in[0], w_rec[0], bias, h_init[0], c_init[0])
        return loss, g_in[None], g_rec[None], g_bias, dh0[None], dc0[None]

    layer_spec = P(('data', 'stage'))
    return jax.shard_map(
        local, mesh=mesh,
        in_specs=(P('data'), P('data'), P('data'), P('stage'), P('stage'), P('stage'), P('stage', 'data'), P('stage', 'data')),
        out_specs=(P('data'), layer_spec, layer_spec, layer_spec, P('stage', 'data'), P('stage', 'data')),
        check_vma=False)
```

time: 7550 us -> 235 us (0.03)
  waiting for transfers between devices: 6270 us -> 0 us
  starting transfers between devices: 800 us -> 0 us
  matrix products: 232 us -> 0 us
  Pallas kernels: 0 us -> 223 us
  other arithmetic: 123 us -> 0 us
  local copies, waits for them, and re-layouts: 92.4 us -> 9.06 us
    ppermute x32 -> x0, waiting for transfers between devices: 6270 us -> none  [the longest x16 5490 us: bwd_tick(): received = lax.ppermute(kept[0], 'stage', down_perm)]
    ppermute x32 -> x0, starting transfers between devices: 800 us -> none  [the longest x16 491 us: fwd_tick(): received = lax.ppermute(kept[0], 'stage', up_perm)]
    dot_general x53 -> x0, matrix products: 232 us -> none  [the longest x32 116 us: cell_step(): jnp.dot(h_prev, w_rec, preferred_element_type=jnp.float32)]
    pallas_call x0 -> x1, Pallas kernels: none -> 223 us  [local(): pl.pallas_call(functools.partial(kernel, last, steps, rows, hidden), out_...]
  transfers between devices with their start and end apart: 32 -> 0, of which waited for: 32 -> 0; matrix products, arithmetic and copies ran while one was open for 0% -> 0% of each run, Pallas kernels for 0% -> 0%
where the time goes in v1:
time: 235 us
  Pallas kernels  223 us (95%)
  local copies, waits for them, and re-layouts  9.06 us (4%)
  between operations  2.35 us (1%)
    pallas_call x1, Pallas kernels, local(): pl.pallas_call(functools.partial(kernel, last, steps, rows, hidden), out_...  223 us
    unnamed x13, local copies, waits for them, and re-layouts  9.06 us

profile of v1, /device:TPU:21, one launch (start us, length us, event | category | flops | bytes accessed | tf_op | source)
XLA Modules:
  0.0 234.5 jit_solution(3168179137595155974)
XLA Ops:
  0.6 223.1 %shard_map.127 = (f32[1]{0:T(128)}, f32[512,2048]{1,0:T(8,128)}, f32[512,2048]{1,0:T(8,128)}, f32[1,2048]{1,0:T(1,128)}, f32[256,512]{1,0:T(8,128)}, /*index=5*/f32[256,512]{1,0:T(8,128)}) custom-call(bf16[4096,512]{1,0:T(8,128)(2,1)} %bitcast.11, bf16[4096,512]{1,0:T(8,128)(2,1)} %bitcast.12, s32[2,128]{1,0:T(2,128)} %bitcast.21, ...), custom_call_target="tpu_custom_call" | custom-call | tf_op jit(solution)/shard_map/pallas_call | solution.py:390
  224.3 0.0 copy-start
  224.3 4.8 %copy.21 = f32[1,512,2048]{2,1,0:T(8,128)} copy(f32[1,512,2048]{2,1,0:T(8,128)} %bitcast.14) | data formatting | bytes 8388608
  229.2 0.0 copy-done
  229.2 0.0 copy-start.3
  229.2 0.0 copy-start.2
  229.2 0.0 copy-start.1
  229.2 2.0 copy.22
  231.2 0.0 copy-done.3
  231.2 0.6 copy.23
  231.8 0.0 copy-done.2
  231.8 0.8 copy.24
  232.6 0.0 copy-done.1
  232.6 0.8 copy.25
Async XLA Ops:
  224.3 4.9 %copy-start = (f32[512,2048]{1,0:T(8,128)S(1)}, f32[512,2048]{1,0:T(8,128)}, u32[]{:S(2)}) copy-start(f32[512,2048]{1,0:T(8,128)} %get-tuple-element.14) | copy-start | bytes 12582916
  229.2 2.0 copy-start.3
  229.2 2.6 %copy-start.2 = (f32[256,512]{1,0:T(8,128)S(1)}, f32[256,512]{1,0:T(8,128)}, u32[]{:S(2)}) copy-start(f32[256,512]{1,0:T(8,128)} %get-tuple-element.16) | copy-start | bytes 1572868
  229.2 3.4 %copy-start.1 = (f32[256,512]{1,0:T(8,128)S(1)}, f32[256,512]{1,0:T(8,128)}, u32[]{:S(2)}) copy-start(f32[256,512]{1,0:T(8,128)} %get-tuple-element.17) | copy-start | bytes 1572868

commit v2 on v1

v2 whole, which is shorter than its diff:
```python
import functools

import jax
import jax.numpy as jnp
from jax import lax
from jax.experimental import pallas as pl
from jax.experimental.pallas import tpu as pltpu
from jax.sharding import PartitionSpec as P

F32 = jnp.float32
BF16 = jnp.bfloat16
COLS = 256
ROWS = 32
B_ROWS = 16
ORDER = (0, 2, 1, 3)
HELD_LIMIT = 47_700_000
FINISH_LIMIT = 16_000_000


def mm(lhs, rhs):
    return jnp.dot(lhs, rhs, preferred_element_type=F32)


def mm_t(lhs, rhs):
    return lax.dot_general(lhs, rhs, (((0,), (0,)), ((), ())), preferred_element_type=F32)


def sigmoid(value):
    return 0.5 * jnp.tanh(0.5 * value) + 0.5


def interleave(main, side):
    done = 0
    for idx, piece in enumerate(main):
        upto = (idx + 1) * len(side) // len(main)
        for other in side[done:upto]:
            other()
        done = upto
        piece()


def kernel(last, steps, rows, hidden,
           inputs_ref, targets_ref, lens_ref, w_in_ref, w_rec_ref, bias_ref, h0_ref, c0_ref,
           partial_ref, dz_1, hist, seq, dhs, dcs, g_bias, loss_buf,
           gates, dz_0, dout, win, wrec, win_t, wrec_t, ring_d, work, ahead, lens, loss_acc, fence,
           f_recv, f_send, b_recv, b_send, loss_recv, loss_send, local_sem, tile_sem):
    stage = lax.axis_index('stage')
    lo, hi = stage > 0, stage < last
    first, top = stage == 0, stage == last
    dz = (dz_0, dz_1)
    batch = 2 * rows
    scale = 1.0 / (batch * steps)

    def at_step(step):
        return pl.ds(pl.multiple_of(step * rows, rows), rows)

    def f_copy(group, step):
        slot = lax.rem(step, 2)
        return pltpu.make_async_remote_copy(
            src_ref=hist.at[group, at_step(steps + 1 + slot), :], dst_ref=seq.at[group, at_step(step), :],
            send_sem=f_send.at[group, slot], recv_sem=f_recv.at[group, step],
            device_id={'stage': stage + 1}, device_id_type=pl.DeviceIdType.MESH)

    def b_copy(group, step):
        slot = lax.rem(step, 2)
        return pltpu.make_async_remote_copy(
            src_ref=ring_d.at[group, slot], dst_ref=dout.at[group, at_step(step), :],
            send_sem=b_send.at[group, slot], recv_sem=b_recv.at[group, step],
            device_id={'stage': stage - 1}, device_id_type=pl.DeviceIdType.MESH)

    def loss_copy():
        return pltpu.make_async_remote_copy(
            src_ref=loss_buf, dst_ref=loss_buf, send_sem=loss_send, recv_sem=loss_recv,
            device_id={'stage': stage - 1}, device_id_type=pl.DeviceIdType.MESH)

    def load(src, dst, sem):
        return pltpu.make_async_copy(src, dst, local_sem.at[sem])

    loads = []
    for q in range(4):
        cols = pl.ds(q * hidden, hidden)
        loads.append(load(w_in_ref.at[:, cols], win.at[q], 0 + q))
        loads.append(load(w_rec_ref.at[:, cols], wrec.at[q], 4 + q))
    loads.append(load(c0_ref.at[pl.ds(0, rows), :], dhs.at[1], 8))
    loads.append(load(c0_ref.at[pl.ds(rows, rows), :], dcs.at[1], 9))
    loads.append(load(c0_ref.at[pl.ds(0, rows), :], dhs.at[0], 10))
    loads.append(load(h0_ref.at[pl.ds(0, rows), :], gates.at[0, :, pl.ds(0, hidden)], 11))
    loads.append(load(h0_ref.at[pl.ds(rows, rows), :], gates.at[1, :, pl.ds(0, hidden)], 12))

    def land(src, group):
        return load(src.at[pl.ds(group * rows * steps, rows * steps), :],
                    dz_0.at[group], 13 + group)

    @pl.when(first)
    def _():
        for group in range(2):
            land(inputs_ref, group).start()

    for copy in loads:
        copy.start()

    @pl.when(top)
    def _():
        for group in range(2):
            land(targets_ref, group).start()

    barrier = pltpu.get_barrier_semaphore()

    @pl.when(lo)
    def _():
        pl.semaphore_signal(barrier, inc=1, device_id={'stage': stage - 1}, device_id_type=pl.DeviceIdType.MESH)

    @pl.when(hi)
    def _():
        pl.semaphore_signal(barrier, inc=1, device_id={'stage': stage + 1}, device_id_type=pl.DeviceIdType.MESH)

    for group in range(2):
        row = lens_ref[group:group + 1, :].astype(F32)
        lens[group] = jnp.broadcast_to(row, (128, rows)).T

    loss_acc[...] = jnp.zeros_like(loss_acc)
    g_bias[...] = jnp.zeros_like(g_bias)

    @pl.when(jnp.logical_and(lo, hi))
    def _():
        pl.semaphore_wait(barrier, 2)

    @pl.when(jnp.logical_or(first, top))
    def _():
        pl.semaphore_wait(barrier, 1)

    def time_major(group, dst):
        size = 16 * steps
        out_row = lax.broadcasted_iota(jnp.int32, (size, size), 0)
        in_row = lax.broadcasted_iota(jnp.int32, (size, size), 1)
        step_of, row_of = lax.div(out_row, 16), lax.rem(out_row, 16)
        permute = (in_row == row_of * steps + step_of).astype(F32).astype(BF16)

        def block(idx, _):
            piece = dz_0[group, pl.ds(pl.multiple_of(idx * size, size), size), :]
            moved = mm(permute, piece).astype(BF16)
            for step in range(steps):
                dst[group, pl.ds(pl.multiple_of(step * rows + idx * 16, 16), 16), :] = moved[step * 16:(step + 1) * 16]
            return 0

        lax.fori_loop(0, rows // 16, block, 0)

    def set_up():
        def turn(q, _):
            win_t[q] = win[q].T
            wrec_t[q] = wrec[q].T
            return 0

        lax.fori_loop(0, 4, turn, 0)

    @pl.when(first)
    def _():
        land(inputs_ref, 0).wait()
        time_major(0, seq)

    for copy in loads:
        copy.wait()
    for group in range(2):
        h_start = gates[group, :, 0:hidden].astype(BF16)
        hist[group, 0:rows, :] = h_start
        hist[group, (steps + 2) * rows:(steps + 3) * rows, :] = h_start

    @pl.when(top)
    def _():
        for group in range(2):
            land(targets_ref, group).wait()
            time_major(group, dout)

    early = stage >= (last + 1) // 2

    @pl.when(early)
    def _():
        set_up()

    def cols_of(block):
        return slice(block * COLS, (block + 1) * COLS)

    def bias_of(q, block):
        return bias_ref[:, q * hidden + block * COLS:q * hidden + (block + 1) * COLS]

    def cell(group, step, z, c_ref, rs, cs, slot=None):
        in_gate, cand = sigmoid(z[0]), jnp.tanh(z[2])
        forget = sigmoid(z[1])
        c_prev = c_ref[rs, cs]
        c_new = forget * c_prev + in_gate * cand
        c_ref[rs, cs] = c_new
        out_gate = sigmoid(z[3])
        if slot is not None:
            for part, value in enumerate((in_gate, forget, cand, out_gate, c_prev)):
                gates[slot, rs, part * hidden + cs.start:part * hidden + cs.stop] = value
        live = jnp.tile(lens[group, rs, :] > step.astype(F32), (1, COLS // 128))
        return jnp.where(live, out_gate * jnp.tanh(c_new), 0.0).astype(BF16)

    def row_blocks():
        return [slice(r, r + ROWS) for r in range(0, rows, ROWS)]

    def forward_old(group, step):
        def piece(block, q):
            cs = cols_of(block)
            h = hist[group, at_step(steps + 2 - lax.rem(step, 2)), :]
            work[:, q * hidden + cs.start:q * hidden + cs.stop] = mm(h, wrec[q, :, cs]) + bias_of(q, block)

        return [functools.partial(piece, block, q) for block in range(hidden // COLS) for q in ORDER]

    def forward_wait(group, step):
        @pl.when(lo)
        def _():
            f_copy(group, step).wait_recv()
            fence[...] = jnp.zeros_like(fence)

        @pl.when(jnp.logical_and(hi, step >= 2))
        def _():
            f_copy(group, step - 2).wait_send()

    def forward_new(group, step, c_ref):
        slot = lax.rem(step, 2)
        x = seq[group, at_step(step), :]
        for block in range(hidden // COLS):
            cs = cols_of(block)
            new = {q: mm(x, win[q, :, cs]) for q in ORDER}
            for rs in row_blocks():
                z = [new[q][rs] + work[rs, q * hidden + cs.start:q * hidden + cs.stop] for q in range(4)]
                at = pl.ds(pl.multiple_of((steps + 1 + slot) * rows + rs.start, ROWS), ROWS)
                hist[group, at, cs] = cell(group, step, z, c_ref, rs, cs)

    def forward_send(group, step):
        @pl.when(hi)
        def _():
            f_copy(group, step).start()

        @pl.when(top)
        def _():
            slot = lax.rem(step, 2)
            for rs in row_blocks():
                at = pl.ds(pl.multiple_of(step * rows + rs.start, ROWS), ROWS)
                live = jnp.tile(lens[group, rs, :] > step.astype(F32), (1, hidden // 128))
                error = jnp.where(live, hist[group, pl.ds(pl.multiple_of((steps + 1 + slot) * rows + rs.start, ROWS), ROWS), :].astype(F32) - dout[group, at, :].astype(F32), 0.0)
                loss_acc[...] += jnp.sum((error * error).reshape(ROWS // 8, 8, hidden), axis=0)
                dout[group, at, :] = (error * scale).astype(BF16)

    def recompute_mm(group, step):
        def piece(block, q):
            cs = cols_of(block)
            x = seq[group, at_step(step), :]
            h = hist[group, at_step(step), :]
            ahead[:, q * hidden + cs.start:q * hidden + cs.stop] = mm(x, win[q, :, cs]) + mm(h, wrec[q, :, cs])

        return [functools.partial(piece, block, q) for block in range(hidden // COLS) for q in ORDER]

    def recompute_cell(group, step, slot, c_ref):
        def piece(block, rs):
            cs = cols_of(block)
            z = [ahead[rs, q * hidden + cs.start:q * hidden + cs.stop] + bias_of(q, block) for q in range(4)]
            at = pl.ds(pl.multiple_of((step + 1) * rows + rs.start, ROWS), ROWS)
            hist[group, at, cs] = cell(group, step, z, c_ref, rs, cs, slot)

        return [functools.partial(piece, block, rs) for block in range(hidden // COLS) for rs in row_blocks()]

    def backward_wait(group, step):
        @pl.when(hi)
        def _():
            b_copy(group, step).wait_recv()
            fence[...] = jnp.zeros_like(fence)

        @pl.when(jnp.logical_and(lo, step < steps - 2))
        def _():
            b_copy(group, step + 2).wait_send()

    def factors(slot):
        def piece(block, r):
            cs = cols_of(block)
            rs = slice(r, r + B_ROWS)
            in_gate, forget, cand, out_gate, c_prev = [
                gates[slot, rs, part * hidden + cs.start:part * hidden + cs.stop] for part in range(5)]
            new, old = in_gate * cand, forget * c_prev
            tanh_c = jnp.tanh(old + new)
            out = out_gate * tanh_c
            values = (new * (1.0 - in_gate), old * (1.0 - forget), in_gate - new * cand, out * (1.0 - out_gate),
                      out_gate - out * tanh_c, forget)
            for part, value in enumerate(values):
                work[rs, part * hidden + cs.start:part * hidden + cs.stop] = value

        return [functools.partial(piece, block, r) for block in range(hidden // COLS) for r in range(0, rows, B_ROWS)]

    def now_rows(q, start, stop):
        base = (steps + 3 + q % 2) * rows
        return slice(base + start, base + stop)

    def backward_cell(group, step):
        for block in range(hidden // COLS):
            cs = cols_of(block)
            sums = [None] * 4
            for r in range(0, rows, B_ROWS):
                rs = slice(r, r + B_ROWS)
                at = pl.ds(pl.multiple_of(step * rows + r, B_ROWS), B_ROWS)
                f = [work[rs, part * hidden + cs.start:part * hidden + cs.stop] for part in range(6)]
                d_h = dhs[group, rs, cs] + dout[group, at, cs].astype(F32)
                d_cell = d_h * f[4] + dcs[group, rs, cs]
                dcs[group, rs, cs] = d_cell * f[5]
                for q, value in enumerate((d_cell * f[0], d_cell * f[1], d_cell * f[2], d_h * f[3])):
                    low = value.astype(BF16)
                    hist[q // 2, now_rows(q, r, r + B_ROWS), cs] = low
                    dz[group][q, at, cs] = low
                    part = jnp.sum(value.reshape(B_ROWS // 8, 8, COLS), axis=0)
                    sums[q] = part if sums[q] is None else sums[q] + part
            for q in range(4):
                g_bias[q, :, cs] += sums[q]

    def through(weights, store):
        held = [None]
        n_blocks = hidden // COLS

        def piece(block, q):
            part = mm(hist[q // 2, now_rows(q, 0, rows), cols_of(block)], weights[q, cols_of(block), :])
            held[0] = part if held[0] is None else held[0] + part
            if block == n_blocks - 1 and q == 3:
                store(held[0])

        return [functools.partial(piece, block, q) for block in range(n_blocks) for q in range(4)]

    def backward_state(group):
        def store(value):
            dhs[group] = value

        return through(wrec_t, store)

    def backward_mm(group, step):
        def store(value):
            ring_d[group, lax.rem(step, 2)] = value.astype(BF16)

        for piece in through(win_t, store):
            piece()

    def backward_send(group, step):
        @pl.when(lo)
        def _():
            b_copy(group, step).start()

    def weight_tile(group, tick):
        q, m = lax.div(tick, 4), lax.rem(tick, 4)
        across = pl.ds(pl.multiple_of(m * (hidden // 4), hidden // 4), hidden // 4)

        def piece(which):
            lhs = seq[group, :, across] if which == 0 else hist[group, 0:steps * rows, across]
            gates[tick, :, which * hidden:(which + 1) * hidden] = mm_t(lhs, dz[group][q])

        return [functools.partial(piece, which) for which in range(2)]

    def tile_copy(tick, which):
        q, m = lax.div(tick, 4), lax.rem(tick, 4)
        part = hidden // 4
        return pltpu.make_async_copy(
            gates.at[tick, :, pl.ds(which * hidden, hidden)],
            partial_ref.at[which, pl.ds(pl.multiple_of(m * part, part), part), pl.ds(pl.multiple_of(q * hidden, hidden), hidden)],
            tile_sem.at[which, tick])

    def phase_1(step, _):
        interleave(forward_old(0, step), [])
        forward_wait(0, step)
        forward_new(0, step, dhs.at[1])
        forward_send(0, step)
        return 0

    lax.fori_loop(0, steps, phase_1, 0)

    @pl.when(first)
    def _():
        land(inputs_ref, 1).wait()
        time_major(1, seq)

    again = load(c0_ref.at[pl.ds(rows, rows), :], dhs.at[1], 8)
    again.start()

    def phase_2(step, _):
        interleave(forward_old(1, step), recompute_cell(0, step, step, dhs.at[0]))
        ahead_step = step + 1
        interleave(recompute_mm(lax.div(ahead_step, steps), lax.rem(ahead_step, steps)), [])
        forward_wait(1, step)
        forward_new(1, step, dcs.at[1])
        forward_send(1, step)
        return 0

    interleave(recompute_mm(0, 0), [])
    lax.fori_loop(0, steps, phase_2, 0)
    again.wait()

    @pl.when(top)
    def _():
        total = jnp.sum(loss_acc[...]) * (0.5 * scale)
        loss_buf[...] = jnp.full(loss_buf.shape, total, F32)
        loss_copy().start()

    @pl.when(jnp.logical_not(early))
    def _():
        set_up()

    dcs[0] = jnp.zeros((rows, hidden), F32)
    for q in range(4):
        hist[q // 2, now_rows(q, 0, rows), :] = jnp.zeros((rows, hidden), BF16)

    def phase_3(tick, _):
        step = steps - 1 - tick
        interleave(backward_state(0), recompute_cell(1, tick, steps - tick, dhs.at[1]))
        interleave(recompute_mm(1, lax.rem(tick + 1, steps)), factors(step))
        backward_wait(0, step)
        backward_cell(0, step)
        backward_mm(0, step)
        backward_send(0, step)
        return 0

    lax.fori_loop(0, steps, phase_3, 0)
    interleave(backward_state(0), [])

    @pl.when(hi)
    def _():
        loss_copy().wait_recv()

        @pl.when(lo)
        def _():
            loss_copy().start()

    dcs[1] = jnp.zeros((rows, hidden), F32)
    for q in range(4):
        hist[q // 2, now_rows(q, 0, rows), :] = jnp.zeros((rows, hidden), BF16)

    def phase_4(tick, _):
        step = steps - 1 - tick

        @pl.when(tick > 0)
        def _():
            for which in range(2):
                tile_copy(tick - 1, which).start()

        interleave(backward_state(1), factors(steps - step))
        interleave(weight_tile(0, tick), [])
        backward_wait(1, step)
        backward_cell(1, step)
        backward_mm(1, step)
        backward_send(1, step)
        return 0

    lax.fori_loop(0, steps, phase_4, 0)
    interleave(backward_state(1), [])
    for which in range(2):
        tile_copy(steps - 1, which).start()

    def tile_wait(tick, _):
        for which in range(2):
            tile_copy(tick, which).wait()
        return 0

    lax.fori_loop(0, steps, tile_wait, 0)

    @pl.when(hi)
    def _():
        for group in range(2):
            for step in (steps - 2, steps - 1):
                f_copy(group, step).wait_send()

    @pl.when(lo)
    def _():
        for group in range(2):
            for step in (1, 0):
                b_copy(group, step).wait_send()
        loss_copy().wait_send()


def finish_kernel(steps, rows, hidden, partial_ref, dz, hist, seq, dhs, dcs, g_bias, loss_buf,
                  loss_ref, g_in_ref, g_rec_ref, g_bias_ref, dh0_ref, dc0_ref, total, in_sem, out_sem, state_sem):
    def take(q, which):
        cols = pl.ds(pl.multiple_of(q * hidden, hidden), hidden)
        return pltpu.make_async_copy(partial_ref.at[which, :, cols], total.at[q, which], in_sem.at[q, which])

    def put(q, which):
        cols = pl.ds(pl.multiple_of(q * hidden, hidden), hidden)
        return pltpu.make_async_copy(total.at[q, which], (g_in_ref, g_rec_ref)[which].at[:, cols], out_sem.at[q, which])

    for q in range(4):
        for which in range(2):
            take(q, which).start()
    states = []
    for group in range(2):
        at = pl.ds(group * rows, rows)
        states.append(pltpu.make_async_copy(dhs.at[group], dh0_ref.at[at, :], state_sem.at[group]))
        states.append(pltpu.make_async_copy(dcs.at[group], dc0_ref.at[at, :], state_sem.at[2 + group]))
    for copy in states:
        copy.start()
    loss_ref[0] = loss_buf[0, 0]
    for q in range(4):
        g_bias_ref[:, q * hidden:(q + 1) * hidden] = jnp.sum(g_bias[q], axis=0, keepdims=True)

    def gate(q, _):
        new = [mm_t(lhs, dz[q]) for lhs in (seq[1], hist[1, 0:steps * rows, :])]
        for which in range(2):
            take(q, which).wait()
        for which in range(2):
            total[q, which] = total[q, which] + new[which]
            put(q, which).start()
        return 0

    lax.fori_loop(0, 4, gate, 0)
    for copy in states:
        copy.wait()
    for q in range(4):
        for which in range(2):
            put(q, which).wait()


def solution(mesh):
    last = mesh.shape['stage'] - 1

    def local(inputs, targets, lengths, w_in, w_rec, bias, h_init, c_init):
        batch, steps, hidden = inputs.shape
        rows = batch // 2
        wide = 4 * hidden
        any_spec = pl.BlockSpec(memory_space=pl.ANY)
        vmem_spec = pl.BlockSpec(memory_space=pltpu.VMEM)
        dma = pltpu.SemaphoreType.DMA
        held = pl.pallas_call(
            functools.partial(kernel, last, steps, rows, hidden),
            out_shape=(
                jax.ShapeDtypeStruct((8, hidden, wide), F32),
                pltpu.VMEM((4, steps * rows, hidden), BF16),
                pltpu.VMEM((2, (steps + 5) * rows, hidden), BF16),
                pltpu.VMEM((2, steps * rows, hidden), BF16),
                pltpu.VMEM((2, rows, hidden), F32),
                pltpu.VMEM((2, rows, hidden), F32),
                pltpu.VMEM((4, 8, hidden), F32),
                pltpu.VMEM((8, 128), F32)),
            in_specs=[any_spec, any_spec, vmem_spec, any_spec, any_spec, vmem_spec, any_spec, any_spec],
            out_specs=(any_spec,) + (vmem_spec,) * 7,
            scratch_shapes=[
                pltpu.VMEM((steps + 1, rows, 5 * hidden), F32),
                pltpu.VMEM((4, steps * rows, hidden), BF16),
                pltpu.VMEM((2, steps * rows, hidden), BF16),
                pltpu.VMEM((4, hidden, hidden), BF16),
                pltpu.VMEM((4, hidden, hidden), BF16),
                pltpu.VMEM((4, hidden, hidden), BF16),
                pltpu.VMEM((4, hidden, hidden), BF16),
                pltpu.VMEM((2, 2, rows, hidden), BF16),
                pltpu.VMEM((rows, 6 * hidden), F32),
                pltpu.VMEM((rows, 4 * hidden), F32),
                pltpu.VMEM((2, rows, 128), F32),
                pltpu.VMEM((8, hidden), F32),
                pltpu.VMEM((8, 128), F32),
                dma((2, steps)), dma((2, 2)), dma((2, steps)), dma((2, 2)), dma, dma, dma((15,)), dma((2, steps))],
            compiler_params=pltpu.CompilerParams(
                collective_id=0, has_side_effects=True, vmem_limit_bytes=HELD_LIMIT),
        )(inputs.reshape(batch * steps, hidden), targets.reshape(batch * steps, hidden), lengths.reshape(2, rows),
          w_in[0], w_rec[0], bias, h_init[0], c_init[0])
        loss, g_in, g_rec, g_bias, dh0, dc0 = pl.pallas_call(
            functools.partial(finish_kernel, steps, rows, hidden),
            out_shape=(
                jax.ShapeDtypeStruct((1,), F32),
                jax.ShapeDtypeStruct((hidden, wide), F32),
                jax.ShapeDtypeStruct((hidden, wide), F32),
                jax.ShapeDtypeStruct((1, wide), F32),
                jax.ShapeDtypeStruct((batch, hidden), F32),
                jax.ShapeDtypeStruct((batch, hidden), F32)),
            in_specs=[pl.BlockSpec(memory_space=pltpu.HBM)] + [vmem_spec] * 7,
            out_specs=(pl.BlockSpec(memory_space=pltpu.SMEM), any_spec, any_spec, vmem_spec, any_spec, any_spec),
            scratch_shapes=[pltpu.VMEM((4, 2, hidden, hidden), F32), dma((4, 2)), dma((4, 2)), dma((4,))],
            compiler_params=pltpu.CompilerParams(vmem_limit_bytes=FINISH_LIMIT),
        )(*held)
        return loss, g_in[None], g_rec[None], g_bias, dh0[None], dc0[None]

    layer_spec = P(('data', 'stage'))
    return jax.shard_map(
        local, mesh=mesh,
        in_specs=(P('data'), P('data'), P('data'), P('stage'), P('stage'), P('stage'), P('stage', 'data'), P('stage', 'data')),
        out_specs=(P('data'), layer_spec, layer_spec, layer_spec, P('stage', 'data'), P('stage', 'data')),
        check_vma=False)
```

time: 235 us -> 215 us (0.915)
  local copies, waits for them, and re-layouts: 9.06 us -> 0 us
  Pallas kernels: 223 us -> 214 us
    pallas_call x1, Pallas kernels: 223 us -> 202 us  [local(): pl.pallas_call(functools.partial(kernel, last, steps, rows, hidden), out_...]
    pallas_call x0 -> x1, Pallas kernels: none -> 12.3 us  [local(): pl.pallas_call(functools.partial(finish_kernel, steps, rows, hidden), out...]
    unnamed x13 -> x0, local copies, waits for them, and re-layouts: 9.06 us -> none
where the time goes in v2:
time: 215 us
  Pallas kernels  214 us (100%)
    pallas_call x1, Pallas kernels, local(): pl.pallas_call(functools.partial(kernel, last, steps, rows, hidden), out_...  202 us
    pallas_call x1, Pallas kernels, local(): pl.pallas_call(functools.partial(finish_kernel, steps, rows, hidden), out...  12.3 us

profile of v2, /device:TPU:21, one launch (start us, length us, event | category | flops | bytes accessed | tf_op | source)
XLA Modules:
  0.0 214.5 jit_solution(5723086912099732114)
XLA Ops:
  0.6 201.6 %shard_map.127 = (f32[8,512,2048]{2,1,0:T(8,128)}, bf16[4,2048,512]{2,1,0:T(8,128)(2,1)S(1)}, bf16[2,2688,512]{2,1,0:T(8,128)(2,1)S(1)}, bf16[2,2048,512]{2,1,0:...) custom-call(bf16[4096,512]{1,0:T(8,128)(2,1)} %bitcast.11, ...), custom_call_target="tpu_custom_call" | custom-call | tf_op jit(solution)/shard_map/pallas_call | solution.py:524
  202.2 12.3 %shard_map.128 = (f32[1]{0:T(128)}, f32[512,2048]{1,0:T(8,128)}, f32[512,2048]{1,0:T(8,128)}, f32[1,2048]{1,0:T(1,128)}, f32[256,512]{1,0:T(8,128)}, /*index=5*/f32[256,512]{1,0:T(8,128)}) custom-call(f32[8,512,2048]{2,1,0:T(8,128)} %get-tuple-element.20.partial_ref, bf16[4,2048,512]{2,1,0:T(8,128)(2,1)S(1)} %get-tuple-element.21.dz, ...), custom_call_target="tpu_custom_call" | custom-call | tf_op jit(solution)/shard_map/pallas_call | solution.py:556

commit v3 on v2

--- a/solution.py
+++ b/solution.py
@@ -13,7 +13,7 @@
 ROWS = 32
 B_ROWS = 16
 ORDER = (0, 2, 1, 3)
-HELD_LIMIT = 47_700_000
+HELD_LIMIT = 48_700_000
 FINISH_LIMIT = 16_000_000
 
 
@@ -42,12 +42,13 @@
 def kernel(last, steps, rows, hidden,
            inputs_ref, targets_ref, lens_ref, w_in_ref, w_rec_ref, bias_ref, h0_ref, c0_ref,
            partial_ref, dz_1, hist, seq, dhs, dcs, g_bias, loss_buf,
-           gates, dz_0, dout, win, wrec, win_t, wrec_t, ring_d, work, ahead, lens, loss_acc, fence,
+           gates, dz_0, now, dout, win_t, wrec_t, ring_h, ring_d, work, lens, loss_acc, fence,
            f_recv, f_send, b_recv, b_send, loss_recv, loss_send, local_sem, tile_sem):
     stage = lax.axis_index('stage')
     lo, hi = stage > 0, stage < last
     first, top = stage == 0, stage == last
     dz = (dz_0, dz_1)
+    win, wrec = dz_1.at[:, pl.ds(0, hidden), :], dz_1.at[:, pl.ds(hidden, hidden), :]
     batch = 2 * rows
     scale = 1.0 / (batch * steps)
 
@@ -57,7 +58,7 @@
     def f_copy(group, step):
         slot = lax.rem(step, 2)
         return pltpu.make_async_remote_copy(
-            src_ref=hist.at[group, at_step(steps + 1 + slot), :], dst_ref=seq.at[group, at_step(step), :],
+            src_ref=ring_h.at[group, slot], dst_ref=seq.at[group, at_step(step), :],
             send_sem=f_send.at[group, slot], recv_sem=f_recv.at[group, step],
             device_id={'stage': stage + 1}, device_id_type=pl.DeviceIdType.MESH)
 
@@ -93,11 +94,14 @@
 
     @pl.when(first)
     def _():
-        for group in range(2):
-            land(inputs_ref, group).start()
+        land(inputs_ref, 0).start()
 
     for copy in loads:
         copy.start()
+
+    @pl.when(first)
+    def _():
+        land(inputs_ref, 1).start()
 
     @pl.when(top)
     def _():
@@ -136,14 +140,15 @@
         step_of, row_of = lax.div(out_row, 16), lax.rem(out_row, 16)
         permute = (in_row == row_of * steps + step_of).astype(F32).astype(BF16)
 
-        def block(idx, _):
-            piece = dz_0[group, pl.ds(pl.multiple_of(idx * size, size), size), :]
-            moved = mm(permute, piece).astype(BF16)
-            for step in range(steps):
-                dst[group, pl.ds(pl.multiple_of(step * rows + idx * 16, 16), 16), :] = moved[step * 16:(step + 1) * 16]
+        def blocks(trip, _):
+            for idx in (trip * 2, trip * 2 + 1):
+                piece = dz_0[group, pl.ds(pl.multiple_of(idx * size, size), size), :]
+                moved = mm(permute, piece).astype(BF16)
+                for step in range(steps):
+                    dst[group, pl.ds(pl.multiple_of(step * rows + idx * 16, 16), 16), :] = moved[step * 16:(step + 1) * 16]
             return 0
 
-        lax.fori_loop(0, rows // 16, block, 0)
+        lax.fori_loop(0, rows // 32, blocks, 0)
 
     def set_up():
         def turn(q, _):
@@ -163,7 +168,7 @@
     for group in range(2):
         h_start = gates[group, :, 0:hidden].astype(BF16)
         hist[group, 0:rows, :] = h_start
-        hist[group, (steps + 2) * rows:(steps + 3) * rows, :] = h_start
+        ring_h[group, 1] = h_start
 
     @pl.when(top)
     def _():
@@ -186,26 +191,30 @@
     def cell(group, step, z, c_ref, rs, cs, slot=None):
         in_gate, cand = sigmoid(z[0]), jnp.tanh(z[2])
         forget = sigmoid(z[1])
-        c_prev = c_ref[rs, cs]
-        c_new = forget * c_prev + in_gate * cand
+        new, old = in_gate * cand, forget * c_ref[rs, cs]
+        c_new = old + new
         c_ref[rs, cs] = c_new
+        tanh_c = jnp.tanh(c_new)
         out_gate = sigmoid(z[3])
+        out = out_gate * tanh_c
         if slot is not None:
-            for part, value in enumerate((in_gate, forget, cand, out_gate, c_prev)):
+            values = (new * (1.0 - in_gate), old * (1.0 - forget), in_gate - new * cand, out * (1.0 - out_gate),
+                      out_gate - out * tanh_c, forget)
+            for part, value in enumerate(values):
                 gates[slot, rs, part * hidden + cs.start:part * hidden + cs.stop] = value
         live = jnp.tile(lens[group, rs, :] > step.astype(F32), (1, COLS // 128))
-        return jnp.where(live, out_gate * jnp.tanh(c_new), 0.0).astype(BF16)
+        return jnp.where(live, out, 0.0).astype(BF16)
 
     def row_blocks():
         return [slice(r, r + ROWS) for r in range(0, rows, ROWS)]
 
     def forward_old(group, step):
-        def piece(block, q):
-            cs = cols_of(block)
-            h = hist[group, at_step(steps + 2 - lax.rem(step, 2)), :]
-            work[:, q * hidden + cs.start:q * hidden + cs.stop] = mm(h, wrec[q, :, cs]) + bias_of(q, block)
-
-        return [functools.partial(piece, block, q) for block in range(hidden // COLS) for q in ORDER]
+        def piece(q):
+            h = ring_h[group, 1 - lax.rem(step, 2)]
+            at = slice(q * hidden, (q + 1) * hidden)
+            work[:, at] = mm(h, wrec[q]) + bias_ref[:, at]
+
+        return [functools.partial(piece, q) for q in ORDER]
 
     def forward_wait(group, step):
         @pl.when(lo)
@@ -220,91 +229,88 @@
     def forward_new(group, step, c_ref):
         slot = lax.rem(step, 2)
         x = seq[group, at_step(step), :]
-        for block in range(hidden // COLS):
+        n_blocks = hidden // COLS
+        order = [(q, block) for block in range(n_blocks) for q in (0, 1, 2)] + [(3, block) for block in range(n_blocks)]
+        new = {(q, block): mm(x, win[q, :, cols_of(block)]) for q, block in order}
+        bent = {}
+
+        def z(q, block, rs):
+            return new[q, block][rs] + work[rs, q * hidden + block * COLS:q * hidden + (block + 1) * COLS]
+
+        for block in range(n_blocks):
             cs = cols_of(block)
-            new = {q: mm(x, win[q, :, cs]) for q in ORDER}
             for rs in row_blocks():
-                z = [new[q][rs] + work[rs, q * hidden + cs.start:q * hidden + cs.stop] for q in range(4)]
-                at = pl.ds(pl.multiple_of((steps + 1 + slot) * rows + rs.start, ROWS), ROWS)
-                hist[group, at, cs] = cell(group, step, z, c_ref, rs, cs)
+                in_gate, cand, forget = sigmoid(z(0, block, rs)), jnp.tanh(z(2, block, rs)), sigmoid(z(1, block, rs))
+                c_new = forget * c_ref[rs, cs] + in_gate * cand
+                c_ref[rs, cs] = c_new
+                bent[block, rs.start] = jnp.tanh(c_new)
+        for block in range(n_blocks):
+            for rs in row_blocks():
+                live = jnp.tile(lens[group, rs, :] > step.astype(F32), (1, COLS // 128))
+                out = sigmoid(z(3, block, rs)) * bent[block, rs.start]
+                ring_h[group, slot, rs, cols_of(block)] = jnp.where(live, out, 0.0).astype(BF16)
 
     def forward_send(group, step):
         @pl.when(hi)
         def _():
             f_copy(group, step).start()
 
-        @pl.when(top)
-        def _():
-            slot = lax.rem(step, 2)
-            for rs in row_blocks():
-                at = pl.ds(pl.multiple_of(step * rows + rs.start, ROWS), ROWS)
-                live = jnp.tile(lens[group, rs, :] > step.astype(F32), (1, hidden // 128))
-                error = jnp.where(live, hist[group, pl.ds(pl.multiple_of((steps + 1 + slot) * rows + rs.start, ROWS), ROWS), :].astype(F32) - dout[group, at, :].astype(F32), 0.0)
-                loss_acc[...] += jnp.sum((error * error).reshape(ROWS // 8, 8, hidden), axis=0)
-                dout[group, at, :] = (error * scale).astype(BF16)
+        if group == 0:
+            @pl.when(top)
+            def _():
+                output_error(group, step, lambda rs: ring_h[group, lax.rem(step, 2), rs, :])
+
+    def output_error(group, step, made):
+        for rs in row_blocks():
+            at = pl.ds(pl.multiple_of(step * rows + rs.start, ROWS), ROWS)
+            live = jnp.tile(lens[group, rs, :] > step.astype(F32), (1, hidden // 128))
+            error = jnp.where(live, made(rs).astype(F32) - dout[group, at, :].astype(F32), 0.0)
+            loss_acc[...] += jnp.sum((error * error).reshape(ROWS // 8, 8, hidden), axis=0)
+            dout[group, at, :] = (error * scale).astype(BF16)
 
     def recompute_mm(group, step):
-        def piece(block, q):
-            cs = cols_of(block)
-            x = seq[group, at_step(step), :]
-            h = hist[group, at_step(step), :]
-            ahead[:, q * hidden + cs.start:q * hidden + cs.stop] = mm(x, win[q, :, cs]) + mm(h, wrec[q, :, cs])
-
-        return [functools.partial(piece, block, q) for block in range(hidden // COLS) for q in ORDER]
-
-    def recompute_cell(group, step, slot, c_ref):
-        def piece(block, rs):
-            cs = cols_of(block)
-            z = [ahead[rs, q * hidden + cs.start:q * hidden + cs.stop] + bias_of(q, block) for q in range(4)]
+        x = seq[group, at_step(step), :]
+        h = hist[group, at_step(step), :]
+        return [{q: mm(x, win[q, :, cols_of(block)]) + mm(h, wrec[q, :, cols_of(block)]) for q in ORDER}
+                for block in range(hidden // COLS)]
+
+    def recompute_cell(group, step, slot, c_ref, new, block):
+        cs = cols_of(block)
+        for rs in row_blocks():
+            z = [new[block][q][rs] + bias_of(q, block) for q in range(4)]
             at = pl.ds(pl.multiple_of((step + 1) * rows + rs.start, ROWS), ROWS)
             hist[group, at, cs] = cell(group, step, z, c_ref, rs, cs, slot)
 
-        return [functools.partial(piece, block, rs) for block in range(hidden // COLS) for rs in row_blocks()]
-
     def backward_wait(group, step):
         @pl.when(hi)
         def _():
             b_copy(group, step).wait_recv()
             fence[...] = jnp.zeros_like(fence)
 
+        if group == 1:
+            @pl.when(top)
+            def _():
+                output_error(group, step, lambda rs: hist[
+                    group, pl.ds(pl.multiple_of((step + 1) * rows + rs.start, ROWS), ROWS), :])
+
         @pl.when(jnp.logical_and(lo, step < steps - 2))
         def _():
             b_copy(group, step + 2).wait_send()
 
-    def factors(slot):
-        def piece(block, r):
-            cs = cols_of(block)
-            rs = slice(r, r + B_ROWS)
-            in_gate, forget, cand, out_gate, c_prev = [
-                gates[slot, rs, part * hidden + cs.start:part * hidden + cs.stop] for part in range(5)]
-            new, old = in_gate * cand, forget * c_prev
-            tanh_c = jnp.tanh(old + new)
-            out = out_gate * tanh_c
-            values = (new * (1.0 - in_gate), old * (1.0 - forget), in_gate - new * cand, out * (1.0 - out_gate),
-                      out_gate - out * tanh_c, forget)
-            for part, value in enumerate(values):
-                work[rs, part * hidden + cs.start:part * hidden + cs.stop] = value
-
-        return [functools.partial(piece, block, r) for block in range(hidden // COLS) for r in range(0, rows, B_ROWS)]
-
-    def now_rows(q, start, stop):
-        base = (steps + 3 + q % 2) * rows
-        return slice(base + start, base + stop)
-
-    def backward_cell(group, step):
+    def backward_cell(group, step, slot):
         for block in range(hidden // COLS):
             cs = cols_of(block)
             sums = [None] * 4
             for r in range(0, rows, B_ROWS):
                 rs = slice(r, r + B_ROWS)
                 at = pl.ds(pl.multiple_of(step * rows + r, B_ROWS), B_ROWS)
-                f = [work[rs, part * hidden + cs.start:part * hidden + cs.stop] for part in range(6)]
+                f = [gates[slot, rs, part * hidden + cs.start:part * hidden + cs.stop] for part in range(6)]
                 d_h = dhs[group, rs, cs] + dout[group, at, cs].astype(F32)
                 d_cell = d_h * f[4] + dcs[group, rs, cs]
                 dcs[group, rs, cs] = d_cell * f[5]
                 for q, value in enumerate((d_cell * f[0], d_cell * f[1], d_cell * f[2], d_h * f[3])):
                     low = value.astype(BF16)
-                    hist[q // 2, now_rows(q, r, r + B_ROWS), cs] = low
+                    now[q, rs, cs] = low
                     dz[group][q, at, cs] = low
                     part = jnp.sum(value.reshape(B_ROWS // 8, 8, COLS), axis=0)
                     sums[q] = part if sums[q] is None else sums[q] + part
@@ -316,7 +322,7 @@
         n_blocks = hidden // COLS
 
         def piece(block, q):
-            part = mm(hist[q // 2, now_rows(q, 0, rows), cols_of(block)], weights[q, cols_of(block), :])
+            part = mm(now[q, :, cols_of(block)], weights[q, cols_of(block), :])
             held[0] = part if held[0] is None else held[0] + part
             if block == n_blocks - 1 and q == 3:
                 store(held[0])
@@ -377,17 +383,68 @@
     again.start()
 
     def phase_2(step, _):
-        interleave(forward_old(1, step), recompute_cell(0, step, step, dhs.at[0]))
-        ahead_step = step + 1
-        interleave(recompute_mm(lax.div(ahead_step, steps), lax.rem(ahead_step, steps)), [])
+        new = recompute_mm(0, step)
+        recompute_cell(0, step, step, dhs.at[0], new, 0)
+        interleave(forward_old(1, step), [])
+        recompute_cell(0, step, step, dhs.at[0], new, 1)
         forward_wait(1, step)
         forward_new(1, step, dcs.at[1])
         forward_send(1, step)
         return 0
 
-    interleave(recompute_mm(0, 0), [])
     lax.fori_loop(0, steps, phase_2, 0)
     again.wait()
+
+    @pl.when(jnp.logical_not(early))
+    def _():
+        set_up()
+
+    def backward(group, step, slot):
+        backward_wait(group, step)
+        backward_cell(group, step, slot)
+        backward_mm(group, step)
+        backward_send(group, step)
+
+    dhs[0] = jnp.zeros((rows, hidden), F32)
+    dcs[0] = jnp.zeros((rows, hidden), F32)
+
+    def phase_3(tick, _):
+        step = steps - 1 - tick
+        backward(0, step, step)
+        new = recompute_mm(1, tick)
+        recompute_cell(1, tick, steps - tick, dhs.at[1], new, 0)
+        interleave(backward_state(0), [])
+        recompute_cell(1, tick, steps - tick, dhs.at[1], new, 1)
+        return 0
+
+    lax.fori_loop(0, steps, phase_3, 0)
+    dhs[1] = jnp.zeros((rows, hidden), F32)
+    dcs[1] = jnp.zeros((rows, hidden), F32)
+
+    def tile_start(tick):
+        for which in range(2):
+            tile_copy(tick, which).start()
+
+    def phase_4(tick, _):
+        step = steps - 1 - tick
+        backward(1, step, steps - step)
+
+        @pl.when(early)
+        def _():
+            interleave(backward_state(1), [])
+
+        @pl.when(jnp.logical_not(early))
+        def _():
+            @pl.when(tick > 0)
+            def _():
+                tile_start(tick - 1)
+
+            interleave(backward_state(1), [])
+            interleave(weight_tile(0, tick), [])
+
+        return 0
+
+    lax.fori_loop(0, steps, phase_4, 0)
 
     @pl.when(top)
     def _():
@@ -395,59 +452,28 @@
         loss_buf[...] = jnp.full(loss_buf.shape, total, F32)
         loss_copy().start()
 
-    @pl.when(jnp.logical_not(early))
-    def _():
-        set_up()
-
-    dcs[0] = jnp.zeros((rows, hidden), F32)
-    for q in range(4):
-        hist[q // 2, now_rows(q, 0, rows), :] = jnp.zeros((rows, hidden), BF16)
-
-    def phase_3(tick, _):
-        step = steps - 1 - tick
-        interleave(backward_state(0), recompute_cell(1, tick, steps - tick, dhs.at[1]))
-        interleave(recompute_mm(1, lax.rem(tick + 1, steps)), factors(step))
-        backward_wait(0, step)
-        backward_cell(0, step)
-        backward_mm(0, step)
-        backward_send(0, step)
+    @pl.when(hi)
+    def _():
+        loss_copy().wait_recv()
+
+        @pl.when(lo)
+        def _():
+            loss_copy().start()
+
+    def late_tile(tick, _):
+        interleave(weight_tile(0, tick), [])
+
+        @pl.when(tick > 0)
+        def _():
+            tile_start(tick - 1)
+
         return 0
 
-    lax.fori_loop(0, steps, phase_3, 0)
-    interleave(backward_state(0), [])
-
-    @pl.when(hi)
-    def _():
-        loss_copy().wait_recv()
-
-        @pl.when(lo)
-        def _():
-            loss_copy().start()
-
-    dcs[1] = jnp.zeros((rows, hidden), F32)
-    for q in range(4):
-        hist[q // 2, now_rows(q, 0, rows), :] = jnp.zeros((rows, hidden), BF16)
-
-    def phase_4(tick, _):
-        step = steps - 1 - tick
-
-        @pl.when(tick > 0)
-        def _():
-            for which in range(2):
-                tile_copy(tick - 1, which).start()
-
-        interleave(backward_state(1), factors(steps - step))
-        interleave(weight_tile(0, tick), [])
-        backward_wait(1, step)
-        backward_cell(1, step)
-        backward_mm(1, step)
-        backward_send(1, step)
-        return 0
-
-    lax.fori_loop(0, steps, phase_4, 0)
-    interleave(backward_state(1), [])
-    for which in range(2):
-        tile_copy(steps - 1, which).start()
+    @pl.when(early)
+    def _():
+        lax.fori_loop(0, steps, late_tile, 0)
+
+    tile_start(steps - 1)
 
     def tile_wait(tick, _):
         for which in range(2):
@@ -526,7 +552,7 @@
             out_shape=(
                 jax.ShapeDtypeStruct((8, hidden, wide), F32),
                 pltpu.VMEM((4, steps * rows, hidden), BF16),
-                pltpu.VMEM((2, (steps + 5) * rows, hidden), BF16),
+                pltpu.VMEM((2, (steps + 1) * rows, hidden), BF16),
                 pltpu.VMEM((2, steps * rows, hidden), BF16),
                 pltpu.VMEM((2, rows, hidden), F32),
                 pltpu.VMEM((2, rows, hidden), F32),
@@ -535,15 +561,14 @@
             in_specs=[any_spec, any_spec, vmem_spec, any_spec, any_spec, vmem_spec, any_spec, any_spec],
             out_specs=(any_spec,) + (vmem_spec,) * 7,
             scratch_shapes=[
-                pltpu.VMEM((steps + 1, rows, 5 * hidden), F32),
+                pltpu.VMEM((steps + 1, rows, 6 * hidden), F32),
                 pltpu.VMEM((4, steps * rows, hidden), BF16),
+                pltpu.VMEM((4, rows, hidden), BF16),
                 pltpu.VMEM((2, steps * rows, hidden), BF16),
                 pltpu.VMEM((4, hidden, hidden), BF16),
                 pltpu.VMEM((4, hidden, hidden), BF16),
-                pltpu.VMEM((4, hidden, hidden), BF16),
-                pltpu.VMEM((4, hidden, hidden), BF16),
                 pltpu.VMEM((2, 2, rows, hidden), BF16),
-                pltpu.VMEM((rows, 6 * hidden), F32),
+                pltpu.VMEM((2, 2, rows, hidden), BF16),
                 pltpu.VMEM((rows, 4 * hidden), F32),
                 pltpu.VMEM((2, rows, 128), F32),
                 pltpu.VMEM((8, hidden), F32),

time: 215 us -> 202 us (0.940)
  Pallas kernels: 214 us -> 201 us
    pallas_call x1, Pallas kernels: 202 us -> 189 us  [local(): pl.pallas_call(functools.partial(kernel, last, steps, rows, hidden), out_...]
where the time goes in v3:
time: 202 us
  Pallas kernels  201 us (100%)
    pallas_call x1, Pallas kernels, local(): pl.pallas_call(functools.partial(kernel, last, steps, rows, hidden), out_...  189 us
    pallas_call x1, Pallas kernels, local(): pl.pallas_call(functools.partial(finish_kernel, steps, rows, hidden), out...  12.3 us

profile of v3, /device:TPU:21, one launch (start us, length us, event | category | flops | bytes accessed | tf_op | source)
XLA Modules:
  0.0 202.0 jit_solution(10241631516884000276)
XLA Ops:
  0.6 189.1 %shard_map.127 = (f32[8,512,2048]{2,1,0:T(8,128)}, bf16[4,2048,512]{2,1,0:T(8,128)(2,1)S(1)}, bf16[2,2176,512]{2,1,0:T(8,128)(2,1)S(1)}, bf16[2,2048,512]{2,1,0:...) custom-call(bf16[4096,512]{1,0:T(8,128)(2,1)} %bitcast.11, ...), custom_call_target="tpu_custom_call" | custom-call | tf_op jit(solution)/shard_map/pallas_call | solution.py:550
  189.7 12.3 %shard_map.128 = (f32[1]{0:T(128)}, f32[512,2048]{1,0:T(8,128)}, f32[512,2048]{1,0:T(8,128)}, f32[1,2048]{1,0:T(1,128)}, f32[256,512]{1,0:T(8,128)}, /*index=5*/f32[256,512]{1,0:T(8,128)}) custom-call(f32[8,512,2048]{2,1,0:T(8,128)} %get-tuple-element.20.partial_ref, bf16[4,2048,512]{2,1,0:T(8,128)(2,1)S(1)} %get-tuple-element.21.dz, ...), custom_call_target="tpu_custom_call" | custom-call | tf_op jit(solution)/shard_map/pallas_call | solution.py:581

commit v4 on v3

--- a/solution.py
+++ b/solution.py
@@ -13,7 +13,7 @@
 ROWS = 32
 B_ROWS = 16
 ORDER = (0, 2, 1, 3)
-HELD_LIMIT = 48_700_000
+HELD_LIMIT = 48_200_000
 FINISH_LIMIT = 16_000_000
 
 
@@ -40,11 +40,13 @@
 
 
 def kernel(last, steps, rows, hidden,
-           inputs_ref, targets_ref, lens_ref, w_in_ref, w_rec_ref, bias_ref, h0_ref, c0_ref,
-           partial_ref, dz_1, hist, seq, dhs, dcs, g_bias, loss_buf,
-           gates, dz_0, now, dout, win_t, wrec_t, ring_h, ring_d, work, lens, loss_acc, fence,
+           inputs_ref, targets_ref, lens_hbm, w_in_ref, w_rec_ref, bias_hbm, h0_ref, c0_ref,
+           partial_ref, dz_1, hist, seq, dhs, dcs, g_bias, loss_buf, last_tile,
+           gates, dz_0, now, dout, win_t, wrec_t, ring_h, ring_d, work, lens, loss_acc, fence, bias_all, lens_all,
            f_recv, f_send, b_recv, b_send, loss_recv, loss_send, local_sem, tile_sem):
     stage = lax.axis_index('stage')
+    bias_ref = bias_all.at[pl.ds(0, 1)]
+    lens_ref = lens_all.at[pl.ds(0, 2)]
     lo, hi = stage > 0, stage < last
     first, top = stage == 0, stage == last
     dz = (dz_0, dz_1)
@@ -77,11 +79,16 @@
     def load(src, dst, sem):
         return pltpu.make_async_copy(src, dst, local_sem.at[sem])
 
+    smalls = [load(lens_hbm, lens_ref, 15), load(bias_hbm, bias_ref, 16)]
+    for copy in smalls:
+        copy.start()
     loads = []
     for q in range(4):
         cols = pl.ds(q * hidden, hidden)
+        loads.append(load(w_rec_ref.at[:, cols], wrec.at[q], 4 + q))
+    for q in range(4):
+        cols = pl.ds(q * hidden, hidden)
         loads.append(load(w_in_ref.at[:, cols], win.at[q], 0 + q))
-        loads.append(load(w_rec_ref.at[:, cols], wrec.at[q], 4 + q))
     loads.append(load(c0_ref.at[pl.ds(0, rows), :], dhs.at[1], 8))
     loads.append(load(c0_ref.at[pl.ds(rows, rows), :], dcs.at[1], 9))
     loads.append(load(c0_ref.at[pl.ds(0, rows), :], dhs.at[0], 10))
@@ -118,20 +125,14 @@
     def _():
         pl.semaphore_signal(barrier, inc=1, device_id={'stage': stage + 1}, device_id_type=pl.DeviceIdType.MESH)
 
+    for copy in smalls:
+        copy.wait()
     for group in range(2):
         row = lens_ref[group:group + 1, :].astype(F32)
         lens[group] = jnp.broadcast_to(row, (128, rows)).T
 
     loss_acc[...] = jnp.zeros_like(loss_acc)
     g_bias[...] = jnp.zeros_like(g_bias)
-
-    @pl.when(jnp.logical_and(lo, hi))
-    def _():
-        pl.semaphore_wait(barrier, 2)
-
-    @pl.when(jnp.logical_or(first, top))
-    def _():
-        pl.semaphore_wait(barrier, 1)
 
     def time_major(group, dst):
         size = 16 * steps
@@ -217,14 +218,14 @@
         return [functools.partial(piece, q) for q in ORDER]
 
     def forward_wait(group, step):
+        @pl.when(jnp.logical_and(hi, step >= 2))
+        def _():
+            f_copy(group, step - 2).wait_send()
+
         @pl.when(lo)
         def _():
             f_copy(group, step).wait_recv()
             fence[...] = jnp.zeros_like(fence)
-
-        @pl.when(jnp.logical_and(hi, step >= 2))
-        def _():
-            f_copy(group, step - 2).wait_send()
 
     def forward_new(group, step, c_ref):
         slot = lax.rem(step, 2)
@@ -243,12 +244,12 @@
                 in_gate, cand, forget = sigmoid(z(0, block, rs)), jnp.tanh(z(2, block, rs)), sigmoid(z(1, block, rs))
                 c_new = forget * c_ref[rs, cs] + in_gate * cand
                 c_ref[rs, cs] = c_new
-                bent[block, rs.start] = jnp.tanh(c_new)
+                live = jnp.tile(lens[group, rs, :] > step.astype(F32), (1, COLS // 128))
+                bent[block, rs.start] = jnp.where(live, 0.5 * jnp.tanh(c_new), 0.0)
         for block in range(n_blocks):
             for rs in row_blocks():
-                live = jnp.tile(lens[group, rs, :] > step.astype(F32), (1, COLS // 128))
-                out = sigmoid(z(3, block, rs)) * bent[block, rs.start]
-                ring_h[group, slot, rs, cols_of(block)] = jnp.where(live, out, 0.0).astype(BF16)
+                out = (jnp.tanh(0.5 * z(3, block, rs)) + 1.0) * bent[block, rs.start]
+                ring_h[group, slot, rs, cols_of(block)] = out.astype(BF16)
 
     def forward_send(group, step):
         @pl.when(hi)
@@ -282,52 +283,66 @@
             hist[group, at, cs] = cell(group, step, z, c_ref, rs, cs, slot)
 
     def backward_wait(group, step):
+        @pl.when(jnp.logical_and(lo, step < steps - 2))
+        def _():
+            b_copy(group, step + 2).wait_send()
+
         @pl.when(hi)
         def _():
             b_copy(group, step).wait_recv()
             fence[...] = jnp.zeros_like(fence)
 
         if group == 1:
-            @pl.when(top)
+            @pl.when(jnp.logical_and(top, step >= steps // 2))
             def _():
-                output_error(group, step, lambda rs: hist[
-                    group, pl.ds(pl.multiple_of((step + 1) * rows + rs.start, ROWS), ROWS), :])
-
-        @pl.when(jnp.logical_and(lo, step < steps - 2))
-        def _():
-            b_copy(group, step + 2).wait_send()
+                for later in (2 * step - steps + 1, 2 * step - steps):
+                    output_error(group, later, lambda rs, later=later: hist[
+                        group, pl.ds(pl.multiple_of((later + 1) * rows + rs.start, ROWS), ROWS), :])
 
     def backward_cell(group, step, slot):
-        for block in range(hidden // COLS):
-            cs = cols_of(block)
+        def part(number, rs, cs):
+            return gates[slot, rs, number * hidden + cs.start:number * hidden + cs.stop]
+
+        def keep(q, value, rs, cs, sums):
+            low = value.astype(BF16)
+            now[q, rs, cs] = low
+            dz[group][q, pl.ds(pl.multiple_of(step * rows + rs.start, B_ROWS), B_ROWS), cs] = low
+            folded = jnp.sum(value.reshape(B_ROWS // 8, 8, COLS), axis=0)
+            sums[q] = folded if sums[q] is None else sums[q] + folded
+
+        blocks = [cols_of(block) for block in range(hidden // COLS)]
+        pieces = [slice(r, r + B_ROWS) for r in range(0, rows, B_ROWS)]
+        for cs in blocks:
             sums = [None] * 4
-            for r in range(0, rows, B_ROWS):
-                rs = slice(r, r + B_ROWS)
-                at = pl.ds(pl.multiple_of(step * rows + r, B_ROWS), B_ROWS)
-                f = [gates[slot, rs, part * hidden + cs.start:part * hidden + cs.stop] for part in range(6)]
+            for rs in pieces:
+                at = pl.ds(pl.multiple_of(step * rows + rs.start, B_ROWS), B_ROWS)
                 d_h = dhs[group, rs, cs] + dout[group, at, cs].astype(F32)
-                d_cell = d_h * f[4] + dcs[group, rs, cs]
-                dcs[group, rs, cs] = d_cell * f[5]
-                for q, value in enumerate((d_cell * f[0], d_cell * f[1], d_cell * f[2], d_h * f[3])):
-                    low = value.astype(BF16)
-                    now[q, rs, cs] = low
-                    dz[group][q, at, cs] = low
-                    part = jnp.sum(value.reshape(B_ROWS // 8, 8, COLS), axis=0)
-                    sums[q] = part if sums[q] is None else sums[q] + part
-            for q in range(4):
+                dhs[group, rs, cs] = d_h
+                keep(3, d_h * part(3, rs, cs), rs, cs, sums)
+            g_bias[3, :, cs] += sums[3]
+        for cs in blocks:
+            sums = [None] * 4
+            for rs in pieces:
+                d_cell = dhs[group, rs, cs] * part(4, rs, cs) + dcs[group, rs, cs]
+                dcs[group, rs, cs] = d_cell * part(5, rs, cs)
+                for q in range(3):
+                    keep(q, d_cell * part(q, rs, cs), rs, cs, sums)
+            for q in range(3):
                 g_bias[q, :, cs] += sums[q]
 
     def through(weights, store):
         held = [None]
         n_blocks = hidden // COLS
 
+        order = [(block, 3) for block in range(n_blocks)] + [(block, q) for block in range(n_blocks) for q in range(3)]
+
         def piece(block, q):
             part = mm(now[q, :, cols_of(block)], weights[q, cols_of(block), :])
             held[0] = part if held[0] is None else held[0] + part
-            if block == n_blocks - 1 and q == 3:
+            if (block, q) == order[-1]:
                 store(held[0])
 
-        return [functools.partial(piece, block, q) for block in range(n_blocks) for q in range(4)]
+        return [functools.partial(piece, block, q) for block, q in order]
 
     def backward_state(group):
         def store(value):
@@ -371,6 +386,14 @@
         forward_new(0, step, dhs.at[1])
         forward_send(0, step)
         return 0
+
+    @pl.when(jnp.logical_and(lo, hi))
+    def _():
+        pl.semaphore_wait(barrier, 2)
+
+    @pl.when(jnp.logical_or(first, top))
+    def _():
+        pl.semaphore_wait(barrier, 1)
 
     lax.fori_loop(0, steps, phase_1, 0)
 
@@ -421,24 +444,46 @@
     dhs[1] = jnp.zeros((rows, hidden), F32)
     dcs[1] = jnp.zeros((rows, hidden), F32)
 
-    def tile_start(tick):
-        for which in range(2):
-            tile_copy(tick, which).start()
+    def tile_copies(tick):
+        @pl.when(tick > 0)
+        def _():
+            for which in range(2):
+                tile_copy(tick - 1, which).start()
+
+        @pl.when(tick > 1)
+        def _():
+            for which in range(2):
+                tile_copy(tick - 2, which).wait()
+
+    def loss_on():
+        @pl.when(top)
+        def _():
+            total = jnp.sum(loss_acc[...]) * (0.5 * scale)
+            loss_buf[...] = jnp.full(loss_buf.shape, total, F32)
+
+        @pl.when(hi)
+        def _():
+            loss_copy().wait_recv()
+
+        @pl.when(lo)
+        def _():
+            loss_copy().start()
 
     def phase_4(tick, _):
         step = steps - 1 - tick
         backward(1, step, steps - step)
 
+        @pl.when(tick == steps - 4)
+        def _():
+            loss_on()
+
         @pl.when(early)
         def _():
             interleave(backward_state(1), [])
 
         @pl.when(jnp.logical_not(early))
         def _():
-            @pl.when(tick > 0)
-            def _():
-                tile_start(tick - 1)
-
+            tile_copies(tick)
             interleave(backward_state(1), [])
             interleave(weight_tile(0, tick), [])
 
@@ -446,41 +491,19 @@
 
     lax.fori_loop(0, steps, phase_4, 0)
 
-    @pl.when(top)
-    def _():
-        total = jnp.sum(loss_acc[...]) * (0.5 * scale)
-        loss_buf[...] = jnp.full(loss_buf.shape, total, F32)
-        loss_copy().start()
-
-    @pl.when(hi)
-    def _():
-        loss_copy().wait_recv()
-
-        @pl.when(lo)
-        def _():
-            loss_copy().start()
-
     def late_tile(tick, _):
+        tile_copies(tick)
         interleave(weight_tile(0, tick), [])
-
-        @pl.when(tick > 0)
-        def _():
-            tile_start(tick - 1)
-
         return 0
 
     @pl.when(early)
     def _():
         lax.fori_loop(0, steps, late_tile, 0)
 
-    tile_start(steps - 1)
-
-    def tile_wait(tick, _):
-        for which in range(2):
-            tile_copy(tick, which).wait()
-        return 0
-
-    lax.fori_loop(0, steps, tile_wait, 0)
+    for which in range(2):
+        last_tile[which] = gates[steps - 1, :, which * hidden:(which + 1) * hidden]
+    for which in range(2):
+        tile_copy(steps - 2, which).wait()
 
     @pl.when(hi)
     def _():
@@ -496,11 +519,14 @@
         loss_copy().wait_send()
 
 
-def finish_kernel(steps, rows, hidden, partial_ref, dz, hist, seq, dhs, dcs, g_bias, loss_buf,
+def finish_kernel(steps, rows, hidden, partial_ref, dz, hist, seq, dhs, dcs, g_bias, loss_buf, last_tile,
                   loss_ref, g_in_ref, g_rec_ref, g_bias_ref, dh0_ref, dc0_ref, total, in_sem, out_sem, state_sem):
-    def take(q, which):
+    part = hidden // 4
+
+    def take(q, which, piece):
         cols = pl.ds(pl.multiple_of(q * hidden, hidden), hidden)
-        return pltpu.make_async_copy(partial_ref.at[which, :, cols], total.at[q, which], in_sem.at[q, which])
+        at = pl.ds(0, 3 * part) if piece == 0 else pl.ds(3 * part, part)
+        return pltpu.make_async_copy(partial_ref.at[which, at, cols], total.at[q, which, at, :], in_sem.at[q, which, piece])
 
     def put(q, which):
         cols = pl.ds(pl.multiple_of(q * hidden, hidden), hidden)
@@ -508,7 +534,9 @@
 
     for q in range(4):
         for which in range(2):
-            take(q, which).start()
+            take(q, which, 0).start()
+            if q < 3:
+                take(q, which, 1).start()
     states = []
     for group in range(2):
         at = pl.ds(group * rows, rows)
@@ -517,13 +545,21 @@
     for copy in states:
         copy.start()
     loss_ref[0] = loss_buf[0, 0]
+    for which in range(2):
+        total[3, which, 3 * part:4 * part, :] = last_tile[which]
     for q in range(4):
         g_bias_ref[:, q * hidden:(q + 1) * hidden] = jnp.sum(g_bias[q], axis=0, keepdims=True)
 
     def gate(q, _):
         new = [mm_t(lhs, dz[q]) for lhs in (seq[1], hist[1, 0:steps * rows, :])]
         for which in range(2):
-            take(q, which).wait()
+            take(q, which, 0).wait()
+
+        @pl.when(q < 3)
+        def _():
+            for which in range(2):
+                take(q, which, 1).wait()
+
         for which in range(2):
             total[q, which] = total[q, which] + new[which]
             put(q, which).start()
@@ -557,9 +593,10 @@
                 pltpu.VMEM((2, rows, hidden), F32),
                 pltpu.VMEM((2, rows, hidden), F32),
                 pltpu.VMEM((4, 8, hidden), F32),
-                pltpu.VMEM((8, 128), F32)),
-            in_specs=[any_spec, any_spec, vmem_spec, any_spec, any_spec, vmem_spec, any_spec, any_spec],
-            out_specs=(any_spec,) + (vmem_spec,) * 7,
+                pltpu.VMEM((8, 128), F32),
+                pltpu.VMEM((2, hidden // 4, hidden), F32)),
+            in_specs=[any_spec] * 8,
+            out_specs=(any_spec,) + (vmem_spec,) * 8,
             scratch_shapes=[
                 pltpu.VMEM((steps + 1, rows, 6 * hidden), F32),
                 pltpu.VMEM((4, steps * rows, hidden), BF16),
@@ -572,8 +609,10 @@
                 pltpu.VMEM((rows, 4 * hidden), F32),
                 pltpu.VMEM((2, rows, 128), F32),
                 pltpu.VMEM((8, hidden), F32),
-                pltpu.VMEM((8, 128), F32),
-                dma((2, steps)), dma((2, 2)), dma((2, steps)), dma((2, 2)), dma, dma, dma((15,)), dma((2, steps))],
+                pltpu.VMEM((32, 128), F32),
+                pltpu.VMEM((8, wide), F32),
+                pltpu.VMEM((32, 128), jnp.int32),
+                dma((2, steps)), dma((2, 2)), dma((2, steps)), dma((2, 2)), dma, dma, dma((17,)), dma((2, steps))],
             compiler_params=pltpu.CompilerParams(
                 collective_id=0, has_side_effects=True, vmem_limit_bytes=HELD_LIMIT),
         )(inputs.reshape(batch * steps, hidden), targets.reshape(batch * steps, hidden), lengths.reshape(2, rows),
@@ -587,9 +626,9 @@
                 jax.ShapeDtypeStruct((1, wide), F32),
                 jax.ShapeDtypeStruct((batch, hidden), F32),
                 jax.ShapeDtypeStruct((batch, hidden), F32)),
-            in_specs=[pl.BlockSpec(memory_space=pltpu.HBM)] + [vmem_spec] * 7,
+            in_specs=[pl.BlockSpec(memory_space=pltpu.HBM)] + [vmem_spec] * 8,
             out_specs=(pl.BlockSpec(memory_space=pltpu.SMEM), any_spec, any_spec, vmem_spec, any_spec, any_spec),
-            scratch_shapes=[pltpu.VMEM((4, 2, hidden, hidden), F32), dma((4, 2)), dma((4, 2)), dma((4,))],
+            scratch_shapes=[pltpu.VMEM((4, 2, hidden, hidden), F32), dma((4, 2, 2)), dma((4, 2)), dma((4,))],
             compiler_params=pltpu.CompilerParams(vmem_limit_bytes=FINISH_LIMIT),
         )(*held)
         return loss, g_in[None], g_rec[None], g_bias, dh0[None], dc0[None]

time: 202 us -> 199 us (0.985)
    pallas_call x1, Pallas kernels: 189 us -> 186 us  [local(): pl.pallas_call(functools.partial(kernel, last, steps, rows, hidden), out_...]
where the time goes in v4:
time: 199 us
  Pallas kernels  199 us (100%)
    pallas_call x1, Pallas kernels, local(): pl.pallas_call(functools.partial(kernel, last, steps, rows, hidden), out_...  186 us
    pallas_call x1, Pallas kernels, local(): pl.pallas_call(functools.partial(finish_kernel, steps, rows, hidden), out...  12.4 us

profile of v4, /device:TPU:21, one launch (start us, length us, event | category | flops | bytes accessed | tf_op | source)
XLA Modules:
  0.0 199.3 jit_solution(15976045135588110416)
XLA Ops:
  0.6 186.3 %shard_map.127 = (f32[8,512,2048]{2,1,0:T(8,128)}, bf16[4,2048,512]{2,1,0:T(8,128)(2,1)S(1)}, bf16[2,2176,512]{2,1,0:T(8,128)(2,1)S(1)}, bf16[2,2048,512]{2,1,0:...) custom-call(bf16[4096,512]{1,0:T(8,128)(2,1)} %bitcast.11, ...), custom_call_target="tpu_custom_call" | custom-call | tf_op jit(solution)/shard_map/pallas_call | solution.py:586
  186.9 12.4 %shard_map.128 = (f32[1]{0:T(128)}, f32[512,2048]{1,0:T(8,128)}, f32[512,2048]{1,0:T(8,128)}, f32[1,2048]{1,0:T(1,128)}, f32[256,512]{1,0:T(8,128)}, /*index=5*/f32[256,512]{1,0:T(8,128)}) custom-call(f32[8,512,2048]{2,1,0:T(8,128)} %get-tuple-element.21.partial_ref, bf16[4,2048,512]{2,1,0:T(8,128)(2,1)S(1)} %get-tuple-element.22.dz, ...), custom_call_target="tpu_custom_call" | custom-call | tf_op jit(solution)/shard_map/pallas_call | solution.py:620

commit v5 on v4

--- a/solution.py
+++ b/solution.py
@@ -90,10 +90,11 @@
         cols = pl.ds(q * hidden, hidden)
         loads.append(load(w_in_ref.at[:, cols], win.at[q], 0 + q))
     loads.append(load(c0_ref.at[pl.ds(0, rows), :], dhs.at[1], 8))
-    loads.append(load(c0_ref.at[pl.ds(rows, rows), :], dcs.at[1], 9))
-    loads.append(load(c0_ref.at[pl.ds(0, rows), :], dhs.at[0], 10))
     loads.append(load(h0_ref.at[pl.ds(0, rows), :], gates.at[0, :, pl.ds(0, hidden)], 11))
-    loads.append(load(h0_ref.at[pl.ds(rows, rows), :], gates.at[1, :, pl.ds(0, hidden)], 12))
+    late_loads = [
+        load(c0_ref.at[pl.ds(rows, rows), :], dcs.at[1], 9),
+        load(c0_ref.at[pl.ds(0, rows), :], dhs.at[0], 10),
+        load(h0_ref.at[pl.ds(rows, rows), :], gates.at[1, :, pl.ds(0, hidden)], 12)]
 
     def land(src, group):
         return load(src.at[pl.ds(group * rows * steps, rows * steps), :],
@@ -103,12 +104,8 @@
     def _():
         land(inputs_ref, 0).start()
 
-    for copy in loads:
+    for copy in loads[8:] + loads[:8]:
         copy.start()
-
-    @pl.when(first)
-    def _():
-        land(inputs_ref, 1).start()
 
     @pl.when(top)
     def _():
@@ -142,14 +139,14 @@
         permute = (in_row == row_of * steps + step_of).astype(F32).astype(BF16)
 
         def blocks(trip, _):
-            for idx in (trip * 2, trip * 2 + 1):
+            for idx in [trip * 4 + sub for sub in range(4)]:
                 piece = dz_0[group, pl.ds(pl.multiple_of(idx * size, size), size), :]
                 moved = mm(permute, piece).astype(BF16)
                 for step in range(steps):
                     dst[group, pl.ds(pl.multiple_of(step * rows + idx * 16, 16), 16), :] = moved[step * 16:(step + 1) * 16]
             return 0
 
-        lax.fori_loop(0, rows // 32, blocks, 0)
+        lax.fori_loop(0, rows // 64, blocks, 0)
 
     def set_up():
         def turn(q, _):
@@ -164,19 +161,24 @@
         land(inputs_ref, 0).wait()
         time_major(0, seq)
 
-    for copy in loads:
+    for copy in loads[8:]:
         copy.wait()
-    for group in range(2):
+
+    def first_state(group):
         h_start = gates[group, :, 0:hidden].astype(BF16)
         hist[group, 0:rows, :] = h_start
         ring_h[group, 1] = h_start
 
+    first_state(0)
+
     @pl.when(top)
     def _():
         for group in range(2):
             land(targets_ref, group).wait()
             time_major(group, dout)
 
+    for copy in loads[:8]:
+        copy.wait()
     early = stage >= (last + 1) // 2
 
     @pl.when(early)
@@ -395,7 +397,17 @@
     def _():
         pl.semaphore_wait(barrier, 1)
 
+    for copy in late_loads:
+        copy.start()
+
+    @pl.when(first)
+    def _():
+        land(inputs_ref, 1).start()
+
     lax.fori_loop(0, steps, phase_1, 0)
+    for copy in late_loads:
+        copy.wait()
+    first_state(1)
 
     @pl.when(first)
     def _():

time: 199 us -> 199 us (level)
  no operation moved by 1% of the time
where the time goes in v5:
time: 199 us
  Pallas kernels  198 us (99%)
    pallas_call x1, Pallas kernels, local(): pl.pallas_call(functools.partial(kernel, last, steps, rows, hidden), out_...  186 us
    pallas_call x1, Pallas kernels, local(): pl.pallas_call(functools.partial(finish_kernel, steps, rows, hidden), out...  12.4 us

profile of v5, /device:TPU:21, one launch (start us, length us, event | category | flops | bytes accessed | tf_op | source)
XLA Modules:
  0.0 198.7 jit_solution(7869504650990843262)
XLA Ops:
  0.6 185.7 %shard_map.127 = (f32[8,512,2048]{2,1,0:T(8,128)}, bf16[4,2048,512]{2,1,0:T(8,128)(2,1)S(1)}, bf16[2,2176,512]{2,1,0:T(8,128)(2,1)S(1)}, bf16[2,2048,512]{2,1,0:...) custom-call(bf16[4096,512]{1,0:T(8,128)(2,1)} %bitcast.11, ...), custom_call_target="tpu_custom_call" | custom-call | tf_op jit(solution)/shard_map/pallas_call | solution.py:598
  186.3 12.4 %shard_map.128 = (f32[1]{0:T(128)}, f32[512,2048]{1,0:T(8,128)}, f32[512,2048]{1,0:T(8,128)}, f32[1,2048]{1,0:T(1,128)}, f32[256,512]{1,0:T(8,128)}, /*index=5*/f32[256,512]{1,0:T(8,128)}) custom-call(f32[8,512,2048]{2,1,0:T(8,128)} %get-tuple-element.21.partial_ref, bf16[4,2048,512]{2,1,0:T(8,128)(2,1)S(1)} %get-tuple-element.22.dz, ...), custom_call_target="tpu_custom_call" | custom-call | tf_op jit(solution)/shard_map/pallas_call | solution.py:632

commit v6 on v5

--- a/solution.py
+++ b/solution.py
@@ -130,6 +130,7 @@
 
     loss_acc[...] = jnp.zeros_like(loss_acc)
     g_bias[...] = jnp.zeros_like(g_bias)
+    dcs[0] = jnp.zeros((rows, hidden), F32)
 
     def time_major(group, dst):
         size = 16 * steps
@@ -441,7 +442,6 @@
         backward_send(group, step)
 
     dhs[0] = jnp.zeros((rows, hidden), F32)
-    dcs[0] = jnp.zeros((rows, hidden), F32)
 
     def phase_3(tick, _):
         step = steps - 1 - tick

time: 199 us -> 199 us (level)
  no operation moved by 1% of the time
where the time goes in v6:
time: 199 us
  Pallas kernels  198 us (99%)
    pallas_call x1, Pallas kernels, local(): pl.pallas_call(functools.partial(kernel, last, steps, rows, hidden), out_...  186 us
    pallas_call x1, Pallas kernels, local(): pl.pallas_call(functools.partial(finish_kernel, steps, rows, hidden), out...  12.4 us

profile of v6, /device:TPU:21, one launch (start us, length us, event | category | flops | bytes accessed | tf_op | source)
XLA Modules:
  0.0 198.7 jit_solution(17717448636798111883)
XLA Ops:
  0.6 185.6 %shard_map.127 = (f32[8,512,2048]{2,1,0:T(8,128)}, bf16[4,2048,512]{2,1,0:T(8,128)(2,1)S(1)}, bf16[2,2176,512]{2,1,0:T(8,128)(2,1)S(1)}, bf16[2,2048,512]{2,1,0:...) custom-call(bf16[4096,512]{1,0:T(8,128)(2,1)} %bitcast.11, ...), custom_call_target="tpu_custom_call" | custom-call | tf_op jit(solution)/shard_map/pallas_call | solution.py:598
  186.3 12.4 %shard_map.128 = (f32[1]{0:T(128)}, f32[512,2048]{1,0:T(8,128)}, f32[512,2048]{1,0:T(8,128)}, f32[1,2048]{1,0:T(1,128)}, f32[256,512]{1,0:T(8,128)}, /*index=5*/f32[256,512]{1,0:T(8,128)}) custom-call(f32[8,512,2048]{2,1,0:T(8,128)} %get-tuple-element.21.partial_ref, bf16[4,2048,512]{2,1,0:T(8,128)(2,1)S(1)} %get-tuple-element.22.dz, ...), custom_call_target="tpu_custom_call" | custom-call | tf_op jit(solution)/shard_map/pallas_call | solution.py:632
